TPU v7x, 512 devices: a whole 4x4x16 slice. The times are simulated.
512 devices in a mesh: space: 32 (over x, y, core), member: 16 (over z).
Axes of the slice: x: 4, y: 4, z: 16, core: 2. Of those that a mesh axis runs over, the one named last changes fastest.
Arguments:
- obs_pert: bfloat16 [80, 65536], P('member', 'space'), may hold values from -6 to 6
- innovation: bfloat16 [65536], P('space'), may hold values from -6 to 6
- obs_prec: bfloat16 [65536], P('space'), may hold values from 1 to 100
- obs_lists: int32 [6144, 256], P('space'), may hold values from 0 to 6143
- loc_weight: bfloat16 [6144, 256], P('space'), may hold values from 0.049804688 to 1
- send_rows: int32 [32, 16, 32], P('space'), may hold values from 0 to 11
- ocean_src: int32 [3072, 2], P('space'), may hold values from 0 to 511, as said below
- ocean_frac: float32 [3072], P('space'), may hold values from 0 to 1
- ocean_ens: bfloat16 [80, 3072, 2048], P(None, 'space', 'member'), may hold values from -6 to 6
Outputs:
- ocean_anal: bfloat16 [80, 3072, 2048], P(None, 'space', 'member')
Inputs may be any that keep to these rules, and one draw needn't show every extreme that they name: `ocean_src`: the two slots of one ocean block differ.
All inputs are finite; a program needn't handle non-finite values.
Results may differ from a plain program's by a relative error of at most 0.0064.
Values may be sent and summed in bfloat16 or wider, within the bound.
No kernel may reach another device: no remote copies, remote signals or barrier semaphores. Data moves between devices by JAX's collectives and lax.ppermute only.
A program may use at most 64 MiB of HBM per device.

v0:
```python
import jax
import jax.numpy as jnp
from jax import lax
from jax.sharding import PartitionSpec as P

ITERS = 12


def padded(cells, sides, width):
    for axis, dim in sides:
        count = lax.axis_size(axis)
        head = lax.slice_in_dim(cells, 0, width, axis=dim)
        tail = lax.slice_in_dim(cells, cells.shape[dim] - width, cells.shape[dim], axis=dim)
        cells = jnp.concatenate(
            [
                lax.ppermute(tail, axis, [(i, (i + 1) % count) for i in range(count)]),
                cells,
                lax.ppermute(head, axis, [((i + 1) % count, i) for i in range(count)]),
            ],
            axis=dim,
        )
    return cells


def copy_for_each(array, axis):
    devices = lax.axis_size(axis)
    return lax.all_to_all(
        jnp.broadcast_to(array[None], (devices, *array.shape)), axis, 0, 0, tiled=True
    )


def joined_along(pieces, dim):
    pieces = jnp.moveaxis(pieces, 0, dim)
    dims = pieces.shape
    return pieces.reshape(*dims[:dim], dims[dim] * dims[dim + 1], *dims[dim + 2 :])


def gather_directly(array, axis, dim):
    pieces = copy_for_each(array, axis)
    return joined_along(pieces, dim)


def transform(local_obs, loc_sel, innov_sel, prec_sel):
    members = local_obs.shape[0]
    obs_f32 = local_obs.astype(jnp.float32)
    obs_weight = loc_sel.astype(jnp.float32) * prec_sel.astype(jnp.float32)
    weighted = obs_f32 * obs_weight[None]
    gram = jnp.einsum("ibl,jbl->bij", weighted, obs_f32, precision=lax.Precision.HIGHEST)
    pulled = jnp.einsum(
        "ibl,bl->bi", weighted, innov_sel.astype(jnp.float32), precision=lax.Precision.HIGHEST
    )
    identity = jnp.eye(members, dtype=jnp.float32)
    precision_mat = (members - 1.0) * identity + gram
    scale_sum = jnp.trace(precision_mat, axis1=1, axis2=2)
    root_start = precision_mat / scale_sum[:, None, None]
    inverse_start = jnp.broadcast_to(identity, precision_mat.shape)

    def newton(iteration, carry):
        root_iter, inverse_iter = carry
        correction = 1.5 * identity - 0.5 * jnp.einsum(
            "bij,bjk->bik", inverse_iter, root_iter, precision=lax.Precision.HIGHEST
        )
        root_next = jnp.einsum(
            "bij,bjk->bik", root_iter, correction, precision=lax.Precision.HIGHEST
        )
        inverse_next = jnp.einsum(
            "bij,bjk->bik", correction, inverse_iter, precision=lax.Precision.HIGHEST
        )
        return (root_next, inverse_next)

    root_iter, inverse_iter = lax.fori_loop(0, ITERS, newton, (root_start, inverse_start))
    spread = jnp.sqrt((members - 1.0) / scale_sum)[:, None, None] * inverse_iter
    half_way = jnp.einsum("bij,bj->bi", inverse_iter, pulled, precision=lax.Precision.HIGHEST)
    mean_weight = (
        jnp.einsum("bij,bj->bi", inverse_iter, half_way, precision=lax.Precision.HIGHEST)
        / scale_sum[:, None]
    )
    return (spread + mean_weight[:, :, None]).astype(jnp.bfloat16)


def apply_weights(ensemble, mixed):
    ens_mean = jnp.mean(ensemble, axis=0, dtype=jnp.float32)
    deviation = (ensemble.astype(jnp.float32) - ens_mean[None]).astype(jnp.bfloat16)
    product = jnp.einsum("jol,oji->iol", deviation, mixed, preferred_element_type=jnp.float32)
    return (ens_mean[None] + product).astype(jnp.bfloat16)


def shards(
    obs_pert,
    innovation,
    obs_prec,
    obs_lists,
    loc_weight,
    send_rows,
    ocean_src,
    ocean_frac,
    ocean_ens,
):
    n_member = lax.axis_size("member")
    n_space = lax.axis_size("space")
    member_idx = lax.axis_index("member")
    tile_obs = obs_pert.shape[1]
    stacked = jnp.stack([innovation, obs_prec])
    pert_rim, info_rim = (
        padded(obs_pert, (("space", 1),), tile_obs),
        padded(stacked, (("space", 1),), tile_obs),
    )
    blocks = obs_lists.shape[0]
    group_len = blocks // n_member
    lists_mine = lax.dynamic_slice_in_dim(obs_lists, member_idx * group_len, group_len, 0)
    loc_mine = lax.dynamic_slice_in_dim(loc_weight, member_idx * group_len, group_len, 0)
    all_members = gather_directly(pert_rim, "member", 0)
    local_obs = all_members[:, lists_mine]
    innov_sel = info_rim[0][lists_mine]
    prec_sel = info_rim[1][lists_mine]
    weights = transform(local_obs, loc_mine, innov_sel, prec_sel)
    row_choice = lax.dynamic_index_in_dim(send_rows[0], member_idx, 0, keepdims=False)
    picked = weights[row_choice]
    arrived = lax.all_to_all(picked, "space", split_axis=0, concat_axis=0, tiled=True)
    mine_one = ocean_src[:, 0] // n_space == member_idx
    mine_two = ocean_src[:, 1] // n_space == member_idx
    coef_one = jnp.where(mine_one, 1.0 - ocean_frac, 0.0)[:, None, None]
    coef_two = jnp.where(mine_two, ocean_frac, 0.0)[:, None, None]
    take_one = arrived[ocean_src[:, 0] % n_space].astype(jnp.float32)
    take_two = arrived[ocean_src[:, 1] % n_space].astype(jnp.float32)
    partial_mix = coef_one * take_one + coef_two * take_two
    mixed = lax.psum(partial_mix, "member").astype(jnp.bfloat16)
    return apply_weights(ocean_ens, mixed)


def solution(mesh):
    return jax.shard_map(
        shards,
        mesh=mesh,
        in_specs=(
            P("member", "space"),
            P("space"),
            P("space"),
            P("space", None),
            P("space", None),
            P("space", None, None),
            P("space", None),
            P("space"),
            P(None, "space", "member"),
        ),
        out_specs=P(None, "space", "member"),
        check_vma=False,
    )
```

profile of v0, /device:TPU:6, one launch (start us, length us, event | category | flops | bytes accessed | tf_op | source)
XLA Modules:
  0.0 276.2 jit_solution(2189907386546934300)
XLA Ops:
  0.0 1.9 collective-permute-start
  1.9 5.8 %collective-permute-start.1 = (bf16[5,2048]{1,0:T(8,128)(2,1)}, bf16[5,2048]{1,0:T(8,128)(2,1)S(1)}, u32[]{:S(2)}, u32[]{:S(2)}) collective-permute-start(bf16[5,2048]{1,0:T(8,128)(2,1)} %param.11), channel_id=1, source_target_pairs={{16,0},{32,16},{48,32},{64,48},{80,64},{96,80},{112,96},{128,112},... | collective-permute-start | bytes 61448 | tf_op jit(solution)/shard_map/ppermute | solution.py:18
  7.7 1.9 collective-permute-done.1
  10.3 1.3 broadcast_in_dim.23
  11.7 15.4 %all-to-all-start = ((bf16[16,5,6144]{2,1,0:T(8,128)(2,1)}), bf16[16,5,6144]{2,1,0:T(8,128)(2,1)}, u32[]{:S(2)}, u32[]{:S(2)}) async-start(bf16[16,5,6144]{2,1,0:T(8,128)(2,1)} %broadcast_in_dim.23), calls=%async_computation | async-start | bytes 3145728 | tf_op jit(solution)/shard_map/all_to_all | solution.py:27
  27.1 1.9 collective-permute-start.2
  29.1 5.8 %collective-permute-start.3 = (bf16[2,2048]{1,0:T(2,128)(2,1)S(1)}, bf16[2,2048]{1,0:T(2,128)(2,1)S(1)}, u32[]{:S(2)}, u32[]{:S(2)}) collective-permute-start(bf16[2,2048]{1,0:T(2,128)(2,1)S(1)} %pad_maximum_fusion.2), channel_id=1, source_target_pairs={{16,0},{32,16},{48,32},{64,48},{80,64},{96,80},{112,96},{128,112},... | collective-permute-start | bytes 24584 | tf_op jit(solution)/shard_map/ppermute | solution.py:18
  40.4 19.4 %gather_fusion.1 = bf16[3072]{0:T(1024)(128)(2,1)S(1)} fusion(bf16[6144]{0:T(1024)(128)(2,1)S(1)} %get-tuple-element.46, s32[3072]{0:T(1024)S(1)} %broadcast_clamp_fusion), kind=kCustom, calls=%fused_computation.1 | custom fusion | bytes 24576 | tf_op jit(solution)/shard_map/gather | solution.py:115
  59.7 19.4 %gather_fusion.2 = bf16[3072]{0:T(1024)(128)(2,1)S(1)} fusion(bf16[6144]{0:T(1024)(128)(2,1)S(1)} %get-tuple-element.45, s32[3072]{0:T(1024)S(1)} %broadcast_clamp_fusion), kind=kCustom, calls=%fused_computation.2 | custom fusion | bytes 24576 | tf_op jit(solution)/shard_map/gather | solution.py:114
  79.7 1.3 convert_multiply_fusion.3
  81.0 19.9 %all-to-all-done = bf16[16,5,6144]{2,1,0:T(8,128)(2,1)} async-done(((bf16[16,5,6144]{2,1,0:T(8,128)(2,1)}), bf16[16,5,6144]{2,1,0:T(8,128)(2,1)}, u32[]{:S(2)}, u32[]{:S(2)}) %all-to-all-start) | async-done | bytes 983072 | tf_op jit(solution)/shard_map/all_to_all | solution.py:27
  100.9 2.4 reshape.58
  103.3 1.8 copy.31
  105.1 11.5 %gather_fusion = bf16[3072,80]{1,0:T(8,128)(2,1)} fusion(bf16[80,6144]{0,1:T(8,128)(2,1)S(1)} %copy.31, s32[3072]{0:T(1024)S(1)} %broadcast_clamp_fusion), kind=kCustom, calls=%fused_computation | custom fusion | bytes 995328 | tf_op jit(solution)/shard_map/gather | solution.py:113
  116.6 1.4 copy.32
  118.1 1.5 select_reduce_fusion
  120.0 32.0 %while.13 = (s32[]{:T(128)}, f32[12,80,80]{1,2,0:T(8,128)S(1)}, f32[12,80,80]{2,1,0:T(8,128)S(1)}, s32[]{:T(128)}) while((s32[]{:T(128)}, f32[12,80,80]{1,2,0:T(8,128)S(1)}, f32[12,80,80]{2,1,0:T(8,128)S(1)}, s32[]{:T(128)}) %tuple.29), condition=%wide.region_3.4_spmd.clone, body=%wide.region_2.3_spmd.clone.sunk | while | flops 221350400 | bytes 4044853 | solution.py:71
  121.7 1.0 convolution_bitcast_fusion.2
  127.0 1.0 convolution_bitcast_fusion.2
  129.7 1.0 convolution_bitcast_fusion.2
  143.0 1.0 convolution_bitcast_fusion.2
  154.7 1.5 gather_fusion.3
  156.2 6.2 %all-to-all-start.1 = ((bf16[32,80,80]{2,1,0:T(8,128)(2,1)}), bf16[32,80,80]{2,1,0:T(8,128)(2,1)S(1)}, u32[]{:S(2)}, u32[]{:S(2)}) async-start(bf16[32,80,80]{2,1,0:T(8,128)(2,1)} %gather_fusion.3), calls=%async_computation.1 | async-start | bytes 1310720 | tf_op jit(solution)/shard_map/all_to_all | solution.py:119
  162.4 1.7 fusion.4
  164.1 8.9 %all-to-all-done.1 = bf16[32,80,80]{2,1,0:T(8,128)(2,1)S(1)} async-done(((bf16[32,80,80]{2,1,0:T(8,128)(2,1)}), bf16[32,80,80]{2,1,0:T(8,128)(2,1)S(1)}, u32[]{:S(2)}, u32[]{:S(2)}) %all-to-all-start.1) | async-done | bytes 409632 | tf_op jit(solution)/shard_map/all_to_all | solution.py:119
  173.9 3.5 %copy.34 = bf16[96,80,80]{0,2,1:T(8,128)(2,1)} copy(bf16[96,80,80]{2,1,0:T(8,128)(2,1)S(1)} %gather_fusion.4) | data formatting | bytes 2457600 | tf_op jit(solution)/shard_map/gather | solution.py:124
  178.3 3.5 %copy.35 = bf16[96,80,80]{0,2,1:T(8,128)(2,1)} copy(bf16[96,80,80]{2,1,0:T(8,128)(2,1)S(1)} %gather_fusion.5) | data formatting | bytes 2457600 | tf_op jit(solution)/shard_map/gather | solution.py:125
  181.8 2.5 multiply_add_fusion
  184.2 81.6 %all-reduce.1 = bf16[96,80,80]{0,2,1:T(8,128)(2,1)} all-reduce(f32[96,80,80]{0,2,1:T(8,128)S(1)} %multiply_add_fusion), channel_id=1, replica_groups=mesh['space'=32,'member'=16] {'member'}, use_global_device_ids=true, to_apply=%region_4.5 | all-reduce | flops 614400 | bytes 3686400 | tf_op jit(solution)/shard_map/psum | solution.py:127
  265.8 5.9 %copy.36 = bf16[96,80,80]{1,2,0:T(8,128)(2,1)S(1)} copy(bf16[96,80,80]{0,2,1:T(8,128)(2,1)} %all-reduce.1) | data formatting | bytes 2457600 | tf_op jit(solution)/shard_map/convert_element_type | solution.py:127
  271.7 2.8 %fusion.6 = bf16[80,96,128]{2,0,1:T(8,128)(2,1)S(1)} fusion(bf16[96,80,80]{1,2,0:T(8,128)(2,1)S(1)} %copy.36, bf16[80,96,128]{2,1,0:T(8,128)(2,1)} %fusion.4, f32[96,128]{1,0:T(8,128)S(1)} %copy-done.2), kind=kOutput, calls=%fused_computation.18 | convolution fusion | flops 159252480 | bytes 5210112 | tf_op jit(solution)/shard_map/jol,oji->iol/dot_general | solution.py:84
  274.4 1.8 copy.38
  (133 shorter events, 39.2 us)
Async XLA Ops:
  0.0 7.7 %collective-permute-start = (bf16[5,2048]{1,0:T(8,128)(2,1)}, bf16[5,2048]{1,0:T(8,128)(2,1)S(1)}, u32[]{:S(2)}, u32[]{:S(2)}) collective-permute-start(bf16[5,2048]{1,0:T(8,128)(2,1)} %param.11), channel_id=1, source_target_pairs={{0,16},{16,32},{32,48},{48,64},{64,80},{80,96},{96,112},{112,128},... | collective-permute-start | bytes 61448 | tf_op jit(solution)/shard_map/ppermute | solution.py:16
  1.9 7.7 %collective-permute-start.1 = (bf16[5,2048]{1,0:T(8,128)(2,1)}, bf16[5,2048]{1,0:T(8,128)(2,1)S(1)}, u32[]{:S(2)}, u32[]{:S(2)}) collective-permute-start(bf16[5,2048]{1,0:T(8,128)(2,1)} %param.11), channel_id=1, source_target_pairs={{16,0},{32,16},{48,32},{64,48},{80,64},{96,80},{112,96},{128,112},... | collective-permute-start | bytes 61448 | tf_op jit(solution)/shard_map/ppermute | solution.py:18
  11.6 15.4 %copy-start.6 = (bf16[2048]{0:T(1024)(128)(2,1)S(1)}, bf16[2048]{0:T(1024)(128)(2,1)}, u32[]{:S(2)}) copy-start(bf16[2048]{0:T(1024)(128)(2,1)} %param.13) | copy-start | bytes 12292
  11.6 15.4 %copy-start.7 = (bf16[2048]{0:T(1024)(128)(2,1)S(1)}, bf16[2048]{0:T(1024)(128)(2,1)}, u32[]{:S(2)}) copy-start(bf16[2048]{0:T(1024)(128)(2,1)} %param.12) | copy-start | bytes 12292
  11.6 26.5 %copy-start = (bf16[80,96,128]{2,1,0:T(8,128)(2,1)S(1)}, bf16[80,96,128]{2,1,0:T(8,128)(2,1)}, u32[]{:S(2)}) copy-start(bf16[80,96,128]{2,1,0:T(8,128)(2,1)} %param.19) | copy-start | bytes 5898244
  11.6 26.8 %copy-start.8 = (s32[96,2]{0,1:T(2,128)S(1)}, s32[96,2]{0,1:T(2,128)}, u32[]{:S(2)}) copy-start(s32[96,2]{0,1:T(2,128)} %param.17) | copy-start | bytes 2308
  11.7 27.4 %copy-start.13 = (f32[96]{0:T(128)S(1)}, f32[96]{0:T(128)}, u32[]{:S(2)}) copy-start(f32[96]{0:T(128)} %param.18) | copy-start | bytes 1156
  11.7 89.2 %all-to-all-start = ((bf16[16,5,6144]{2,1,0:T(8,128)(2,1)}), bf16[16,5,6144]{2,1,0:T(8,128)(2,1)}, u32[]{:S(2)}, u32[]{:S(2)}) async-start(bf16[16,5,6144]{2,1,0:T(8,128)(2,1)} %broadcast_in_dim.23), calls=%async_computation | async-start | bytes 3145728 | tf_op jit(solution)/shard_map/all_to_all | solution.py:27
  27.1 13.0 %collective-permute-start.2 = (bf16[2,2048]{1,0:T(2,128)(2,1)S(1)}, bf16[2,2048]{1,0:T(2,128)(2,1)S(1)}, u32[]{:S(2)}, u32[]{:S(2)}) collective-permute-start(bf16[2,2048]{1,0:T(2,128)(2,1)S(1)} %pad_maximum_fusion.2), channel_id=1, source_target_pairs={{0,16},{16,32},{32,48},{48,64},{64,80},{80,96},{96,112},{112,128},... | collective-permute-start | bytes 24584 | tf_op jit(solution)/shard_map/ppermute | solution.py:16
  29.1 11.1 %collective-permute-start.3 = (bf16[2,2048]{1,0:T(2,128)(2,1)S(1)}, bf16[2,2048]{1,0:T(2,128)(2,1)S(1)}, u32[]{:S(2)}, u32[]{:S(2)}) collective-permute-start(bf16[2,2048]{1,0:T(2,128)(2,1)S(1)} %pad_maximum_fusion.2), channel_id=1, source_target_pairs={{16,0},{32,16},{48,32},{64,48},{80,64},{96,80},{112,96},{128,112},... | collective-permute-start | bytes 24584 | tf_op jit(solution)/shard_map/ppermute | solution.py:18
  118.0 1.9 copy-start.3
  120.0 32.0 %copy-start.4 = (f32[12,256]{1,0:T(8,128)S(1)}, f32[12,256]{1,0:T(8,128)}, u32[]{:S(2)}) copy-start(f32[12,256]{1,0:T(8,128)} %convert_multiply_fusion.3) | copy-start | bytes 36868
  120.0 32.0 %copy-start.5 = (bf16[12,256,1]{1,2,0:T(2,128)(2,1)S(1)}, bf16[12,256,1]{1,2,0:T(2,128)(2,1)}, u32[]{:S(2)}) copy-start(bf16[12,256,1]{1,2,0:T(2,128)(2,1)} %reshape.121) | copy-start | bytes 18436
  153.5 8.9 %copy-start.11 = (s32[96]{0:T(128)S(1)}, s32[96]{0:T(128)}, u32[]{:S(2)}) copy-start(s32[96]{0:T(128)} %get-tuple-element.55) | copy-start | bytes 1156
  153.5 8.9 %copy-start.12 = (s32[96]{0:T(128)S(1)}, s32[96]{0:T(128)}, u32[]{:S(2)}) copy-start(s32[96]{0:T(128)} %get-tuple-element.56) | copy-start | bytes 1156
  153.5 9.0 %copy-start.1 = (f32[96,128]{1,0:T(8,128)S(1)}, f32[96,128]{1,0:T(8,128)}, u32[]{:S(2)}) copy-start(f32[96,128]{1,0:T(8,128)} %broadcast_multiply_fusion) | copy-start | bytes 147460
  156.2 16.8 %all-to-all-start.1 = ((bf16[32,80,80]{2,1,0:T(8,128)(2,1)}), bf16[32,80,80]{2,1,0:T(8,128)(2,1)S(1)}, u32[]{:S(2)}, u32[]{:S(2)}) async-start(bf16[32,80,80]{2,1,0:T(8,128)(2,1)} %gather_fusion.3), calls=%async_computation.1 | async-start | bytes 1310720 | tf_op jit(solution)/shard_map/all_to_all | solution.py:119
  178.3 3.5 %copy-start.9 = (f32[96]{0:T(128)S(1)}, f32[96]{0:T(128)}, u32[]{:S(2)}) copy-start(f32[96]{0:T(128)} %get-tuple-element.53) | copy-start | bytes 1156
  178.3 3.5 %copy-start.10 = (f32[96]{0:T(128)S(1)}, f32[96]{0:T(128)}, u32[]{:S(2)}) copy-start(f32[96]{0:T(128)} %get-tuple-element.54) | copy-start | bytes 1156
  265.8 5.9 %copy-start.2 = (f32[96,128]{1,0:T(8,128)S(1)}, f32[96,128]{1,0:T(8,128)}, u32[]{:S(2)}) copy-start(f32[96,128]{1,0:T(8,128)} %broadcast_multiply_fusion) | copy-start | bytes 147460
where the time goes:
time: 277 us; the launch traced here: 276 us
  blocking collectives  81.6 us (29%)
  local copies, waits for them, and re-layouts  76.9 us (28%)
  matrix products  37 us (13%)
  starting transfers between devices  36.9 us (13%)
  waiting for transfers between devices  30.6 us (11%)
  other arithmetic  12.1 us (4%)
    psum x1, blocking collectives, shards(): mixed = lax.psum(partial_mix, 'member').astype(jnp.bfloat16)  81.6 us
    gather x2, local copies, waits for them, and re-layouts, shards(): innov_sel = info_rim[0][lists_mine]  20 us
    all_to_all x1, waiting for transfers between devices, copy_for_each(): lax.all_to_all(jnp.broadcast_to(array[None], (devices, *array.shape)), ax...  19.9 us
    gather x1, local copies, waits for them, and re-layouts, shards(): prec_sel = info_rim[1][lists_mine]  19.4 us
    all_to_all x1, starting transfers between devices, copy_for_each(): lax.all_to_all(jnp.broadcast_to(array[None], (devices, *array.shape)), ax...  15.4 us
    gather x2, local copies, waits for them, and re-layouts, shards(): local_obs = all_members[:, lists_mine]  12.9 us
    dot_general x12, matrix products, newton(): jnp.einsum('bij,bjk->bik', root_iter, correction, precision=lax.Precision...  11.7 us
    ppermute x2, starting transfers between devices, padded(): lax.ppermute(head, axis, [((i + 1) % count, i) for i in range(count)])  11.5 us
  transfers between devices with their start and end apart: 6, of which 3 were waited for; matrix products, arithmetic and copies ran while one was open for 17% of the time, Pallas kernels for 0%

commit v1 on v0

v1 whole, which is shorter than its diff:
```python
import jax
import jax.numpy as jnp
from jax import lax
from jax.experimental import pallas as pl
from jax.experimental.pallas import tpu as pltpu
from jax.sharding import PartitionSpec as P

ITERS = 12
LANES = 128
HALF = 16


def iota2(shape, dim):
    return lax.broadcasted_iota(jnp.int32, shape, dim)


def split(x):
    high = x.astype(jnp.bfloat16)
    low = (x - high.astype(jnp.float32)).astype(jnp.bfloat16)
    return high, low


def mm(x, y):
    (xh, xl), (yh, yl) = x, y
    dot = lambda a, b: jnp.dot(a, b, preferred_element_type=jnp.float32)
    return dot(xh, yl) + dot(xl, yh) + dot(xh, yh)


def transform_body(
    lists, loc, left, own, right, out, table, rows, rh, rl, zh, zl, mh, ml, side, wide, packed, packed2
):
    group, local = lists.shape
    tile = own.shape[0]
    members = rh.shape[1]
    for i, part in enumerate((left, own, right)):
        table[pl.ds(i * tile, tile), :] = part[...].astype(jnp.float32)
    eye = (iota2((members, members), 0) == iota2((members, members), 1)).astype(jnp.float32)
    step = 16

    for a in range(group):

        def pull(i, carry, a=a):
            for u in range(step):
                spot = lists[a, i * step + u]
                rows[a, pl.ds(i * step + u, 1), :] = table[pl.ds(spot, 1), :]
            return carry

        lax.fori_loop(0, local // step, pull, 0)
    for a in range(group):
        y = rows[a]
        weight = loc[:, a : a + 1] * y[:, members + 1 : members + 2]
        high, low = split(y * weight)
        y16 = y.astype(jnp.bfloat16)
        dims = (((0,), (0,)), ((), ()))
        gram = lax.dot_general(y16, low, dims, preferred_element_type=jnp.float32)
        gram += lax.dot_general(y16, high, dims, preferred_element_type=jnp.float32)
        mat = gram[:members, :members] + (members - 1.0) * eye
        trace = jnp.sum(
            jnp.sum(mat * eye, axis=1, keepdims=True), axis=0, keepdims=True
        )
        side[a, 0:1, :] = gram[members : members + 1, :]
        side[a, 1:2, :] = jnp.broadcast_to(trace, (1, LANES))
        start = mat / trace
        r = split(start)
        m = split(1.5 * eye - 0.5 * start)
        rh[a], rl[a] = split(mm(r, m))
        zh[a], zl[a] = m

    def newton(i, carry):
        for a in range(group):
            corr = 1.5 * eye - 0.5 * mm((zh[a], zl[a]), (rh[a], rl[a]))
            mh[a], ml[a] = split(corr)
        for a in range(group):
            m = (mh[a], ml[a])
            rh[a], rl[a] = split(mm((rh[a], rl[a]), m))
            zh[a], zl[a] = split(mm(m, (zh[a], zl[a])))
        return carry

    lax.fori_loop(0, ITERS - 2, newton, 0)
    packed[...] = jnp.zeros(packed.shape, jnp.float32)
    packed2[...] = jnp.zeros(packed.shape, jnp.float32)
    lane = iota2((2 * HALF, LANES), 1)
    row = iota2((HALF, LANES), 0)
    for a in range(group):
        z = (zh[a], zl[a])
        corr = 1.5 * eye - 0.5 * mm(z, (rh[a], rl[a]))
        inverse = mm(split(corr), z)
        trace = side[a, 1:2, :members]
        pulled = side[a, 0:1, :members]
        half_way = jnp.sum(inverse * pulled, axis=1, keepdims=True)
        mean_weight = jnp.sum(inverse * half_way, axis=0, keepdims=True) / trace
        wide[0:members, 0:members] = inverse * jnp.sqrt((members - 1.0) / trace)
        wide[members : members + 1, 0:members] = mean_weight
        body = jnp.where(lane < 80, wide[48:80, :], pltpu.roll(wide[16:48, :], 80, 1))
        corner = pltpu.roll(wide[0:16, :], 64, 1)
        mean_rows = jnp.broadcast_to(wide[80:81, :], (HALF, LANES))
        lane_top = lane[:HALF]
        top = jnp.where((lane_top >= 64) & (lane_top < 80), corner, body[:HALF])
        for k in range(5):
            moved = pltpu.roll(mean_rows, 112 - 16 * k, 1)
            top = jnp.where((lane_top >= 112) & (row == k), moved, top)
        packed[pl.ds(a, HALF, stride=16), :] = top
        packed2[pl.ds(a, HALF, stride=16), :] = body[HALF:]
    out[:, 0:LANES] = packed[...].astype(jnp.bfloat16)
    out[:, LANES : 2 * LANES] = packed2[...].astype(jnp.bfloat16)


def transforms(lists, loc_cols, left, own, right, members):
    group, local = lists.shape
    tile = own.shape[0]
    f32, b16 = jnp.float32, jnp.bfloat16
    vmem = pl.BlockSpec(memory_space=pltpu.VMEM)
    small = (group, members, members)
    return pl.pallas_call(
        transform_body,
        out_shape=jax.ShapeDtypeStruct((16 * 16, 2 * LANES), b16),
        in_specs=[pl.BlockSpec(memory_space=pltpu.SMEM), vmem, vmem, vmem, vmem],
        out_specs=vmem,
        scratch_shapes=[
            pltpu.VMEM((3 * tile, LANES), f32),
            pltpu.VMEM((group, local, LANES), f32),
            pltpu.VMEM(small, b16),
            pltpu.VMEM(small, b16),
            pltpu.VMEM(small, b16),
            pltpu.VMEM(small, b16),
            pltpu.VMEM(small, b16),
            pltpu.VMEM(small, b16),
            pltpu.VMEM((group, 8, LANES), f32),
            pltpu.VMEM((88, LANES), f32),
            pltpu.VMEM((16 * 16, LANES), f32),
            pltpu.VMEM((16 * 16, LANES), f32),
        ],
        name="transforms",
    )(lists, loc_cols, left, own, right)


def apply_body(pieces, ens, out, ens32, mix32, mix32b, out32):
    members, blocks = ens.shape[0], ens.shape[1]
    wide = ens[...].astype(jnp.float32)
    mean = jnp.sum(wide, axis=0) * (1.0 / members)
    ens32[...] = wide.reshape(members * blocks, LANES)
    mix32[...] = pieces[:, :, 0:LANES].astype(jnp.float32).reshape(16 * blocks, LANES)
    mix32b[...] = pieces[:, :, LANES:].astype(jnp.float32).reshape(16 * blocks, LANES)
    lane = iota2((members, LANES), 1)
    row = iota2((members, LANES), 0)
    lane8 = iota2((8, LANES), 1)
    row8 = iota2((8, LANES), 0)
    for o in range(blocks):
        first = mix32[pl.ds(o, 16, stride=blocks), :]
        second = mix32b[pl.ds(o, 16, stride=blocks), :]
        pack = jnp.concatenate([first, second], axis=0)
        flip = jnp.transpose(jnp.concatenate([pack, jnp.zeros((96, LANES), jnp.float32)], axis=0))
        lower = jnp.concatenate(
            [pltpu.roll(first, 64, 1), pltpu.roll(pack, 48, 1), pack], axis=0
        )
        right = pltpu.roll(flip[:80], 48, 1)
        inner = pltpu.roll(flip[80:], 16, 1)
        upper = jnp.concatenate(
            [jnp.where(lane[:48] < 48, inner, right[:48]), right[48:]], axis=0
        )
        spread = jnp.where((lane <= row) | (lane < 16), lower, upper)
        means = pltpu.roll(first[:8], 16, 1, stride=16, stride_axis=0)
        means = jnp.where(lane8 // 16 == row8, means, 0.0)
        means = jnp.sum(means, axis=0, keepdims=True)
        weights = (spread + means).astype(jnp.bfloat16)[:, :members]
        base = mean[o : o + 1, :]
        dev = (ens32[pl.ds(o, members, stride=blocks), :] - base).astype(jnp.bfloat16)
        product = jnp.dot(weights, dev, preferred_element_type=jnp.float32)
        out32[pl.ds(o, members, stride=blocks), :] = base + product
    out[...] = out32[...].reshape(members, blocks, LANES).astype(jnp.bfloat16)


def apply_weights(pieces, ensemble):
    members, blocks, cells = ensemble.shape
    step = 16
    f32 = jnp.float32
    return pl.pallas_call(
        apply_body,
        grid=(blocks // step,),
        out_shape=jax.ShapeDtypeStruct(ensemble.shape, jnp.bfloat16),
        in_specs=[
            pl.BlockSpec((16, step, 2 * LANES), lambda i: (0, i, 0)),
            pl.BlockSpec((members, step, cells), lambda i: (0, i, 0)),
        ],
        out_specs=pl.BlockSpec((members, step, cells), lambda i: (0, i, 0)),
        scratch_shapes=[
            pltpu.VMEM((members * step, LANES), f32),
            pltpu.VMEM((16 * step, LANES), f32),
            pltpu.VMEM((16 * step, LANES), f32),
            pltpu.VMEM((members * step, LANES), f32),
        ],
        name="apply",
    )(pieces, ensemble)


def shards(
    obs_pert,
    innovation,
    obs_prec,
    obs_lists,
    loc_weight,
    send_rows,
    ocean_src,
    ocean_frac,
    ocean_ens,
):
    n_member = lax.axis_size("member")
    n_space = lax.axis_size("space")
    member_idx = lax.axis_index("member")
    own_members, tile_obs = obs_pert.shape
    members = own_members * n_member
    chunks = tile_obs // LANES
    b16 = jnp.bfloat16

    flat = obs_pert.reshape(own_members * chunks, LANES)
    spread = lax.all_to_all(
        jnp.broadcast_to(flat[None], (n_member, *flat.shape)), "member", 0, 0, tiled=True
    )
    by_obs = spread.reshape(n_member, own_members, chunks, LANES).transpose(2, 3, 0, 1)
    by_obs = by_obs.reshape(tile_obs, members)
    own = jnp.concatenate(
        [
            by_obs,
            innovation[:, None],
            obs_prec[:, None],
            jnp.zeros((tile_obs, LANES - members - 2), b16),
        ],
        axis=1,
    )
    left = lax.ppermute(own, "space", [(i, (i + 1) % n_space) for i in range(n_space)])
    right = lax.ppermute(own, "space", [((i + 1) % n_space, i) for i in range(n_space)])

    group = obs_lists.shape[0] // n_member
    lists_mine = lax.dynamic_slice_in_dim(obs_lists, member_idx * group, group, 0)
    loc_mine = lax.dynamic_slice_in_dim(loc_weight, member_idx * group, group, 0)
    loc_cols = loc_mine.astype(jnp.float32).T
    pieces = transforms(lists_mine, loc_cols, left, own, right, members)

    arrived_one = lax.all_to_all(
        pieces.reshape(n_member, 16, 2 * LANES), "member", 0, 0, tiled=True
    ).reshape(n_member * 16, 2 * LANES)
    choice = (send_rows[0] + 16 * jnp.arange(n_member, dtype=jnp.int32)[:, None]).T.reshape(-1)
    pick = (choice[:, None] == jnp.arange(n_member * 16, dtype=jnp.int32)[None]).astype(b16)
    chosen = jnp.dot(pick, arrived_one, preferred_element_type=jnp.float32).astype(b16)
    arrived = lax.all_to_all(
        chosen.reshape(n_space, n_member, 2 * LANES), "space", 0, 0, tiled=True
    ).reshape(n_space * n_member, 2 * LANES)
    slot = (ocean_src % n_space) * n_member + ocean_src // n_space
    places = jnp.arange(n_space * n_member, dtype=jnp.int32)[None]
    frac = ocean_frac[:, None]
    coef = jnp.where(slot[:, :1] == places, 1.0 - frac, 0.0) + jnp.where(
        slot[:, 1:] == places, frac, 0.0
    )
    mixed = jnp.dot(
        coef, arrived.astype(jnp.float32), precision=lax.Precision.HIGHEST
    ).astype(b16)
    everything = lax.all_gather(mixed, "member", axis=0, tiled=False)
    return apply_weights(everything, ocean_ens)


def solution(mesh):
    return jax.shard_map(
        shards,
        mesh=mesh,
        in_specs=(
            P("member", "space"),
            P("space"),
            P("space"),
            P("space", None),
            P("space", None),
            P("space", None, None),
            P("space", None),
            P("space"),
            P(None, "space", "member"),
        ),
        out_specs=P(None, "space", "member"),
        check_vma=False,
    )
```

time: 277 us -> 164 us (0.59)
  local copies, waits for them, and re-layouts: 76.9 us -> 6.55 us
  blocking collectives: 81.6 us -> 35.3 us
  Pallas kernels: 0 us -> 36.3 us
  matrix products: 37 us -> 1.31 us
  waiting for transfers between devices: 30.6 us -> 46.5 us
  other arithmetic: 12.1 us -> 1.26 us
    psum x1 -> x0, blocking collectives: 81.6 us -> none  [shards(): mixed = lax.psum(partial_mix, 'member').astype(jnp.bfloat16)]
    gather x10 -> x0, local copies, waits for them, and re-layouts: 62.5 us -> none  [the longest x2 20 us: shards(): innov_sel = info_rim[0][lists_mine]]
    pallas_call x0 -> x2, Pallas kernels: none -> 36.3 us  [the longest x1 27.8 us: transforms(): pl.pallas_call(transform_body, out_shape=jax.ShapeDtypeStruct((16 * 16, 2...]
    dot_general x41 -> x2, matrix products: 37 us -> 1.31 us  [the longest x1 0.98 us: shards(): jnp.dot(pick, arrived_one, preferred_element_type=jnp.float32).astype(b16)]
    all_gather x0 -> x1, blocking collectives: none -> 35.3 us  [shards(): everything = lax.all_gather(mixed, 'member', axis=0, tiled=False)]
    ppermute x4 -> x2, starting transfers between devices: 15.3 us -> 4.46 us  [the longest x1 2.41 us: shards(): lax.ppermute(own, 'space', [(i, (i + 1) % n_space) for i in range(n_space)])]
    all_to_all x2 -> x3, waiting for transfers between devices: 28.8 us -> 38.5 us  [the longest x1 18.7 us: shards(): lax.all_to_all(jnp.broadcast_to(flat[None], (n_member, *flat.shape)), 'me...]
    all_to_all x2 -> x3, starting transfers between devices: 21.6 us -> 31.2 us  [the longest x1 15.2 us: shards(): lax.all_to_all(jnp.broadcast_to(flat[None], (n_member, *flat.shape)), 'me...]
  transfers between devices with their start and end apart: 6 -> 5, of which waited for: 3 -> 5; matrix products, arithmetic and copies ran while one was open for 17% -> 3% of each run, Pallas kernels for 0% -> 0%
where the time goes in v1:
time: 164 us; the launch traced here: 163 us
  waiting for transfers between devices  46.5 us (28%)
  Pallas kernels  36.3 us (22%)
  starting transfers between devices  35.6 us (22%)
  blocking collectives  35.3 us (22%)
  local copies, waits for them, and re-layouts  6.55 us (4%)
    all_gather x1, blocking collectives, shards(): everything = lax.all_gather(mixed, 'member', axis=0, tiled=False)  35.3 us
    pallas_call x1, Pallas kernels, transforms(): pl.pallas_call(transform_body, out_shape=jax.ShapeDtypeStruct((16 * 16, 2...  27.8 us
    all_to_all x1, waiting for transfers between devices, shards(): lax.all_to_all(jnp.broadcast_to(flat[None], (n_member, *flat.shape)), 'me...  18.7 us
    all_to_all x1, starting transfers between devices, shards(): lax.all_to_all(jnp.broadcast_to(flat[None], (n_member, *flat.shape)), 'me...  15.2 us
    all_to_all x1, waiting for transfers between devices, shards(): lax.all_to_all(pieces.reshape(n_member, 16, 2 * LANES), 'member', 0, 0, t...  12.8 us
    all_to_all x1, starting transfers between devices, shards(): lax.all_to_all(pieces.reshape(n_member, 16, 2 * LANES), 'member', 0, 0, t...  8.67 us
    pallas_call x1, Pallas kernels, apply_weights(): pl.pallas_call(apply_body, grid=(blocks // step,), out_shape=jax.ShapeDty...  8.53 us
    all_to_all x1, starting transfers between devices, shards(): lax.all_to_all(chosen.reshape(n_space, n_member, 2 * LANES), 'space', 0,...  7.3 us
  transfers between devices with their start and end apart: 5, of which 5 were waited for; matrix products, arithmetic and copies ran while one was open for 3% of the time, Pallas kernels for 0%

profile of v1, /device:TPU:6, one launch (start us, length us, event | category | flops | bytes accessed | tf_op | source)
XLA Modules:
  0.0 163.0 jit_solution(17271373123970555905)
XLA Ops:
  0.0 0.8 broadcast_in_dim.41
  0.8 0.8 broadcast_in_dim.42
  1.6 15.2 %all-to-all-start = ((bf16[16,80,128]{2,1,0:T(8,128)(2,1)}), bf16[16,80,128]{2,1,0:T(8,128)(2,1)S(1)}, u32[]{:S(2)}, u32[]{:S(2)}) async-start(bf16[16,80,128]{2,1,0:T(8,128)(2,1)} %broadcast_in_dim.42), calls=%async_computation | async-start | bytes 655360 | tf_op jit(solution)/shard_map/all_to_all | solution.py:216
  16.8 1.0 broadcast_in_dim.46
  17.8 1.0 broadcast_in_dim.47
  18.9 0.1 pad.3.clone
  19.0 18.7 %all-to-all-done = bf16[16,80,128]{2,1,0:T(8,128)(2,1)S(1)} async-done(((bf16[16,80,128]{2,1,0:T(8,128)(2,1)}), bf16[16,80,128]{2,1,0:T(8,128)(2,1)S(1)}, u32[]{:S(2)}, u32[]{:S(2)}) %all-to-all-start) | async-done | bytes 327712 | tf_op jit(solution)/shard_map/all_to_all | solution.py:216
  37.7 0.1 copy.19
  37.8 0.3 copy.13
  38.0 0.0 copy-start.4
  38.1 0.5 maximum_maximum_fusion.own
  38.6 2.1 %collective-permute-start.1 = (bf16[2048,128]{1,0:T(8,128)(2,1)S(1)}, bf16[2048,128]{1,0:T(8,128)(2,1)S(1)}, u32[]{:S(2)}, u32[]{:S(2)}) collective-permute-start(bf16[2048,128]{1,0:T(8,128)(2,1)S(1)} %maximum_maximum_fusion.own), channel_id=1, source_target_pairs={{16,0},{32,16},{48,32},{64,48},{80,64},{96,80},{112,96},{128,112},... | collective-permute-start | bytes 1572872 | tf_op jit(solution)/shard_map/ppermute | solution.py:231
  40.7 2.4 %collective-permute-start = (bf16[2048,128]{1,0:T(8,128)(2,1)S(1)}, bf16[2048,128]{1,0:T(8,128)(2,1)S(1)}, u32[]{:S(2)}, u32[]{:S(2)}) collective-permute-start(bf16[2048,128]{1,0:T(8,128)(2,1)S(1)} %maximum_maximum_fusion.own), channel_id=1, source_target_pairs={{0,16},{16,32},{32,48},{48,64},{64,80},{80,96},{96,112},{112,128},... | collective-permute-start | bytes 1572872 | tf_op jit(solution)/shard_map/ppermute | solution.py:230
  43.1 0.7 constant_dynamic-slice_fusion
  43.8 0.1 copy.16
  44.0 0.6 constant_dynamic-slice_fusion.1.lists
  44.6 0.7 convert_bitcast_fusion.loc
  45.2 2.1 %collective-permute-done.1.right = bf16[2048,128]{1,0:T(8,128)(2,1)S(1)} collective-permute-done((bf16[2048,128]{1,0:T(8,128)(2,1)S(1)}, bf16[2048,128]{1,0:T(8,128)(2,1)S(1)}, u32[]{:S(2)}, u32[]{:S(2)}) %collective-permute-start.1) | collective-permute-done | bytes 524320 | tf_op jit(solution)/shard_map/ppermute | solution.py:231
  47.4 5.9 %collective-permute-done.left = bf16[2048,128]{1,0:T(8,128)(2,1)S(1)} collective-permute-done((bf16[2048,128]{1,0:T(8,128)(2,1)S(1)}, bf16[2048,128]{1,0:T(8,128)(2,1)S(1)}, u32[]{:S(2)}, u32[]{:S(2)}) %collective-permute-start) | collective-permute-done | bytes 524320 | tf_op jit(solution)/shard_map/ppermute | solution.py:230
  53.3 0.8 copy-done.3
  54.1 27.8 %transforms.1 = bf16[256,256]{1,0:T(8,128)(2,1)} custom-call(s32[12,256]{1,0:T(8,128)} %constant_dynamic-slice_fusion.1.lists, f32[256,12]{1,0:T(8,128)} %convert_bitcast_fusion.loc, bf16[2048,128]{1,0:T(8,128)(2,1)} %copy-done.3, bf16[2048,128]{1,0:T(8,128)(2,1)} %copy-done.1, bf16[2048,128]{1,0:T(8,128)(2,1)} %copy-done.2), custom_call_target="tpu_custom_call" | custom-call | tf_op jit(solution)/shard_map/transforms/pallas_call | solution.py:114
  81.9 8.7 %all-to-all-start.1 = ((bf16[16,16,256]{2,1,0:T(8,128)(2,1)}), bf16[16,16,256]{2,1,0:T(8,128)(2,1)S(1)}, u32[]{:S(2)}, u32[]{:S(2)}) async-start(bf16[16,16,256]{2,1,0:T(8,128)(2,1)} %bitcast.32), calls=%async_computation.1 | async-start | bytes 262144 | tf_op jit(solution)/shard_map/all_to_all | solution.py:239
  90.5 0.1 fusion.9
  90.6 0.1 copy.11
  90.7 0.1 eq.55
  90.8 12.8 %all-to-all-done.1 = bf16[16,16,256]{2,1,0:T(8,128)(2,1)S(1)} async-done(((bf16[16,16,256]{2,1,0:T(8,128)(2,1)}), bf16[16,16,256]{2,1,0:T(8,128)(2,1)S(1)}, u32[]{:S(2)}, u32[]{:S(2)}) %all-to-all-start.1) | async-done | bytes 131104 | tf_op jit(solution)/shard_map/all_to_all | solution.py:239
  103.6 1.0 convolution_convert_fusion
  104.6 7.3 %all-to-all-start.2 = ((bf16[32,16,256]{2,1,0:T(8,128)(2,1)}), bf16[32,16,256]{2,1,0:T(8,128)(2,1)S(1)}, u32[]{:S(2)}, u32[]{:S(2)}) async-start(bf16[32,16,256]{2,1,0:T(8,128)(2,1)} %bitcast.9), calls=%async_computation.2 | async-start | bytes 524288 | tf_op jit(solution)/shard_map/all_to_all | solution.py:245
  112.0 6.9 %all-to-all-done.2 = bf16[32,16,256]{2,1,0:T(8,128)(2,1)S(1)} async-done(((bf16[32,16,256]{2,1,0:T(8,128)(2,1)}), bf16[32,16,256]{2,1,0:T(8,128)(2,1)S(1)}, u32[]{:S(2)}, u32[]{:S(2)}) %all-to-all-start.2) | async-done | bytes 262176 | tf_op jit(solution)/shard_map/all_to_all | solution.py:245
  118.9 0.3 convolution_convert_fusion.1
  119.2 35.3 %all-gather = bf16[1536,256]{1,0:T(8,128)(2,1)} all-gather(bf16[96,256]{1,0:T(8,128)(2,1)S(1)} %convolution_convert_fusion.1), channel_id=2, replica_groups=mesh['space'=32,'member'=16] {'member'}, dimensions={0}, use_global_device_ids=true | all-gather | bytes 835584 | tf_op jit(solution)/shard_map/all_gather | solution.py:257
  154.5 8.5 %apply.1 = bf16[80,96,128]{2,1,0:T(8,128)(2,1)} custom-call(bf16[16,96,256]{2,1,0:T(8,128)(2,1)} %bitcast.29, bf16[80,96,128]{2,1,0:T(8,128)(2,1)} %ens.1), custom_call_target="tpu_custom_call" | custom-call | tf_op jit(solution)/shard_map/apply/pallas_call | solution.py:177
  (17 shorter events, 0.1 us)
Async XLA Ops:
  0.0 44.0 %copy-start = (s32[192,256]{1,0:T(8,128)S(1)}, s32[192,256]{1,0:T(8,128)}, u32[]{:S(2)}) copy-start(s32[192,256]{1,0:T(8,128)} %param.12) | copy-start | bytes 589828
  1.6 36.1 %all-to-all-start = ((bf16[16,80,128]{2,1,0:T(8,128)(2,1)}), bf16[16,80,128]{2,1,0:T(8,128)(2,1)S(1)}, u32[]{:S(2)}, u32[]{:S(2)}) async-start(bf16[16,80,128]{2,1,0:T(8,128)(2,1)} %broadcast_in_dim.42), calls=%async_computation | async-start | bytes 655360 | tf_op jit(solution)/shard_map/all_to_all | solution.py:216
  38.0 52.5 %copy-start.4 = (s32[1,16,32]{2,1,0:T(8,128)S(1)}, s32[1,16,32]{2,1,0:T(8,128)}, u32[]{:S(2)}) copy-start(s32[1,16,32]{2,1,0:T(8,128)} %param.14) | copy-start | bytes 6148
  38.1 52.7 %copy-start.5 = (s32[96,2]{0,1:T(2,128)S(1)}, s32[96,2]{0,1:T(2,128)}, u32[]{:S(2)}) copy-start(s32[96,2]{0,1:T(2,128)} %param.15) | copy-start | bytes 2308
  38.6 14.7 %copy-start.1 = (bf16[2048,128]{1,0:T(8,128)(2,1)}, bf16[2048,128]{1,0:T(8,128)(2,1)S(1)}, u32[]{:S(2)}) copy-start(bf16[2048,128]{1,0:T(8,128)(2,1)S(1)} %maximum_maximum_fusion.own) | copy-start | bytes 1572868
  38.6 73.3 %copy-start.6 = (f32[96]{0:T(128)S(1)}, f32[96]{0:T(128)}, u32[]{:S(2)}) copy-start(f32[96]{0:T(128)} %param.16) | copy-start | bytes 1156
  38.6 8.7 %collective-permute-start.1 = (bf16[2048,128]{1,0:T(8,128)(2,1)S(1)}, bf16[2048,128]{1,0:T(8,128)(2,1)S(1)}, u32[]{:S(2)}, u32[]{:S(2)}) collective-permute-start(bf16[2048,128]{1,0:T(8,128)(2,1)S(1)} %maximum_maximum_fusion.own), channel_id=1, source_target_pairs={{16,0},{32,16},{48,32},{64,48},{80,64},{96,80},{112,96},{128,112},... | collective-permute-start | bytes 1572872 | tf_op jit(solution)/shard_map/ppermute | solution.py:231
  40.7 12.6 %collective-permute-start = (bf16[2048,128]{1,0:T(8,128)(2,1)S(1)}, bf16[2048,128]{1,0:T(8,128)(2,1)S(1)}, u32[]{:S(2)}, u32[]{:S(2)}) collective-permute-start(bf16[2048,128]{1,0:T(8,128)(2,1)S(1)} %maximum_maximum_fusion.own), channel_id=1, source_target_pairs={{0,16},{16,32},{32,48},{48,64},{64,80},{80,96},{96,112},{112,128},... | collective-permute-start | bytes 1572872 | tf_op jit(solution)/shard_map/ppermute | solution.py:230
  47.4 5.9 %copy-start.2 = (bf16[2048,128]{1,0:T(8,128)(2,1)}, bf16[2048,128]{1,0:T(8,128)(2,1)S(1)}, u32[]{:S(2)}) copy-start(bf16[2048,128]{1,0:T(8,128)(2,1)S(1)} %collective-permute-done.1.right) | copy-start | bytes 1572868
  53.3 0.8 copy-start.3
  81.9 21.8 %all-to-all-start.1 = ((bf16[16,16,256]{2,1,0:T(8,128)(2,1)}), bf16[16,16,256]{2,1,0:T(8,128)(2,1)S(1)}, u32[]{:S(2)}, u32[]{:S(2)}) async-start(bf16[16,16,256]{2,1,0:T(8,128)(2,1)} %bitcast.32), calls=%async_computation.1 | async-start | bytes 262144 | tf_op jit(solution)/shard_map/all_to_all | solution.py:239
  104.6 14.2 %all-to-all-start.2 = ((bf16[32,16,256]{2,1,0:T(8,128)(2,1)}), bf16[32,16,256]{2,1,0:T(8,128)(2,1)S(1)}, u32[]{:S(2)}, u32[]{:S(2)}) async-start(bf16[32,16,256]{2,1,0:T(8,128)(2,1)} %bitcast.9), calls=%async_computation.2 | async-start | bytes 524288 | tf_op jit(solution)/shard_map/all_to_all | solution.py:245

commit v2 on v1

v2 whole, which is shorter than its diff:
```python
import jax
import jax.numpy as jnp
from jax import lax
from jax.experimental import pallas as pl
from jax.experimental.pallas import tpu as pltpu
from jax.sharding import PartitionSpec as P

ITERS = 12
LANES = 128
HALF = 16


def iota2(shape, dim):
    return lax.broadcasted_iota(jnp.int32, shape, dim)


def split(x):
    high = x.astype(jnp.bfloat16)
    low = (x - high.astype(jnp.float32)).astype(jnp.bfloat16)
    return high, low


def as_left(x):
    lane = iota2(x.shape, 1)
    high = x.astype(jnp.bfloat16).astype(jnp.float32)
    low = pltpu.roll(x - high, 80, 1)
    again = pltpu.roll(high, 32, 1)
    first = jnp.where(lane < 80, high, low)
    second = jnp.where(lane < 32, low, again)
    return jnp.concatenate([first.astype(jnp.bfloat16), second.astype(jnp.bfloat16)], axis=1)


def as_right(x):
    high, low = split(x)
    return jnp.concatenate([high, high, low, jnp.zeros((16, x.shape[1]), jnp.bfloat16)], axis=0)


def product(left, right):
    return jnp.dot(left, right, preferred_element_type=jnp.float32)


def transform_body(
    lists, loc, left, own, right, out, table, rows, rl, rr, zl, zr, ml, mr, side, packed
):
    group, local = loc.shape
    tile = own.shape[0]
    members = rl.shape[1]
    for i, part in enumerate((left, own, right)):
        table[pl.ds(i * tile, tile), :] = part[...].astype(jnp.float32)
    eye = (iota2((members, LANES), 0) == iota2((members, LANES), 1)).astype(jnp.float32)
    inside = iota2((members, LANES), 1) < members
    step = 32
    batch = 4

    def pull(i, carry):
        for u in range(step):
            spot = lists[i * step + u]
            rows[pl.ds(i * step + u, 1), :] = table[pl.ds(spot, 1), :]
        return carry

    lax.fori_loop(0, group * local // step, pull, 0)

    def begin(i, carry):
        for k in range(batch):
            a = i * batch + k
            y = rows[pl.ds(a * local, local), :]
            turned = jnp.transpose(y)[:88]
            weight = loc[pl.ds(a, 1), :] * turned[members + 1 : members + 2]
            high, low = split(turned * weight)
            y16 = y.astype(jnp.bfloat16)
            gram = product(low, y16) + product(high, y16)
            mat = jnp.where(inside, gram[:members], 0.0) + (members - 1.0) * eye
            trace = jnp.sum(
                jnp.sum(mat * eye, axis=0, keepdims=True), axis=1, keepdims=True
            )
            side[a, 0:1, :] = gram[members : members + 1, :]
            side[a, 1:2, :] = jnp.broadcast_to(trace, (1, LANES))
            start = mat / trace
            corr = 1.5 * eye - 0.5 * start
            right = as_right(corr)
            zl[a], zr[a] = as_left(corr), right
            root = product(as_left(start), right)
            rl[a], rr[a] = as_left(root), as_right(root)
        return carry

    lax.fori_loop(0, group // batch, begin, 0)

    def newton(i, carry):
        for a in range(group):
            corr = 1.5 * eye - 0.5 * product(zl[a], rr[a])
            ml[a], mr[a] = as_left(corr), as_right(corr)
        for a in range(group):
            root = product(rl[a], mr[a])
            inverse = product(ml[a], zr[a])
            rl[a], rr[a] = as_left(root), as_right(root)
            zl[a], zr[a] = as_left(inverse), as_right(inverse)
        return carry

    lax.fori_loop(0, ITERS - 2, newton, 0)
    lane = iota2((2 * HALF, LANES), 1)
    row8 = iota2((8, LANES), 0)

    def finish(i, carry):
        for k in range(batch):
            a = i * batch + k
            corr = 1.5 * eye - 0.5 * product(zl[a], rr[a])
            inverse = product(as_left(corr), zr[a])
            trace = side[a, 1:2, :]
            half_way = jnp.sum(
                jnp.where(inside, inverse * side[a, 0:1, :], 0.0), axis=1, keepdims=True
            )
            mean_weight = jnp.sum(inverse * half_way, axis=0, keepdims=True) / trace
            spread = inverse * jnp.sqrt((members - 1.0) / trace)
            body = jnp.where(lane < 80, spread[48:80], pltpu.roll(spread[16:48], 80, 1))
            corner = pltpu.roll(spread[0:16], 64, 1)
            mean_rows = jnp.broadcast_to(mean_weight, (8, LANES))
            moved = jnp.zeros((8, LANES), jnp.float32)
            for p in range(5):
                moved = jnp.where(row8 == p, pltpu.roll(mean_rows, 112 - 16 * p, 1), moved)
            lane_top = lane[:HALF]
            top = jnp.where((lane_top >= 64) & (lane_top < 80), corner, body[:HALF])
            mean_top = jnp.where((lane[:8] >= 112) & (row8 < 5), moved, top[:8])
            top = jnp.concatenate([mean_top, top[8:]], axis=0)
            packed[pl.ds(a, HALF, stride=2 * group), :] = top
            packed[pl.ds(group + a, HALF, stride=2 * group), :] = body[HALF:]
        return carry

    lax.fori_loop(0, group // batch, finish, 0)
    out[...] = packed[...].astype(jnp.bfloat16)


def transforms(lists, loc, left, own, right, members):
    group, local = loc.shape
    lists = lists.reshape(-1)
    tile = own.shape[0]
    f32, b16 = jnp.float32, jnp.bfloat16
    vmem = pl.BlockSpec(memory_space=pltpu.VMEM)
    low_high = pltpu.VMEM((group, members, 2 * LANES), b16)
    stacked = pltpu.VMEM((group, 2 * LANES, LANES), b16)
    return pl.pallas_call(
        transform_body,
        out_shape=jax.ShapeDtypeStruct((HALF * 2 * group, LANES), b16),
        in_specs=[pl.BlockSpec(memory_space=pltpu.SMEM), vmem, vmem, vmem, vmem],
        out_specs=vmem,
        scratch_shapes=[
            pltpu.VMEM((3 * tile, LANES), f32),
            pltpu.VMEM((group * local, LANES), f32),
            low_high,
            stacked,
            low_high,
            stacked,
            low_high,
            stacked,
            pltpu.VMEM((group, 8, LANES), f32),
            pltpu.VMEM((HALF * 2 * group, LANES), f32),
        ],
        name="transforms",
    )(lists, loc, left, own, right)


def deviation_body(ens, dev, mean, ens32):
    members, blocks = ens.shape[0], ens.shape[1]
    wide = ens[...].astype(jnp.float32)
    center = jnp.sum(wide, axis=0) * (1.0 / members)
    mean[...] = center
    ens32[...] = (wide - center[None]).reshape(members * blocks, LANES)
    for o in range(blocks):
        dev[o] = ens32[pl.ds(o, members, stride=blocks), :].astype(jnp.bfloat16)


def deviations(ensemble):
    members, blocks, cells = ensemble.shape
    step = 16
    return pl.pallas_call(
        deviation_body,
        grid=(blocks // step,),
        out_shape=(
            jax.ShapeDtypeStruct((blocks, members, cells), jnp.bfloat16),
            jax.ShapeDtypeStruct((blocks, cells), jnp.float32),
        ),
        in_specs=[pl.BlockSpec((members, step, cells), lambda i: (0, i, 0))],
        out_specs=(
            pl.BlockSpec((step, members, cells), lambda i: (i, 0, 0)),
            pl.BlockSpec((step, cells), lambda i: (i, 0)),
        ),
        scratch_shapes=[pltpu.VMEM((members * step, LANES), jnp.float32)],
        name="deviations",
    )(ensemble)


def apply_body(pieces, pieces2, dev, mean, out, mix32, mix32b, out32):
    members, blocks = out.shape[0], out.shape[1]
    mix32[...] = pieces[...].astype(jnp.float32).reshape(16 * blocks, LANES)
    mix32b[...] = pieces2[...].astype(jnp.float32).reshape(16 * blocks, LANES)
    lane = iota2((16, LANES), 1)
    row = iota2((16, LANES), 0)
    lane8, row8 = lane[:8], row[:8]
    zero = jnp.zeros((16, LANES), jnp.float32)
    none = jnp.zeros((16, LANES), jnp.bfloat16)
    keep = lambda low, high, x: jnp.where((lane >= low) & (lane < high), x, 0.0)

    for g in range(blocks // 4):
        packs = []
        for k in range(4):
            packs.append(mix32[pl.ds(4 * g + k, 16, stride=blocks), :])
            packs.append(mix32b[pl.ds(4 * g + k, 16, stride=blocks), :])
        flip = jnp.transpose(jnp.concatenate(packs, axis=0))
        for k in range(4):
            o = 4 * g + k
            first, second = packs[2 * k], packs[2 * k + 1]
            at = 32 * k
            inner_at = (32, 0, 32, 0)[k]
            corner_at = (64, 64, 96, 64)[k]
            inner = pltpu.roll(flip[80:112], (inner_at - at) % LANES, 1)
            corner = pltpu.roll(first, 32, 1) if corner_at == 96 else first
            means = pltpu.roll(first[:8], 16, 1, stride=16, stride_axis=0)
            means = jnp.where((lane8 // 16 == row8) & (row8 < 5), means, 0.0)
            means = jnp.sum(means, axis=0, keepdims=True)
            means = jnp.where(row == 0, jnp.broadcast_to(means, row.shape), 0.0)
            direct = [
                zero,
                keep(80, 112, first),
                keep(80, 128, second[:16]),
                keep(0, 64, first),
                keep(0, 80, second),
                means,
            ]
            turned = [
                keep(at, at + 32, flip[0:16])
                + keep(inner_at, inner_at + 32, inner[:16])
                + keep(corner_at, corner_at + 16, corner),
                keep(at, at + 32, flip[16:32]) + keep(inner_at + 16, inner_at + 32, inner[16:]),
                keep(at, at + 32, flip[32:48]),
                keep(at + 16, at + 32, flip[48:64]),
                zero,
                zero,
            ]
            weights = jnp.concatenate(
                [
                    jnp.concatenate(direct, axis=0).astype(jnp.bfloat16),
                    jnp.concatenate(turned, axis=0).astype(jnp.bfloat16),
                ],
                axis=1,
            )
            d = dev[o]
            outer, middle, start = d[48:80], d[16:48], d[0:16]
            tail = (
                [outer, middle, start, none, none, none],
                [middle, outer, start, none, none, none],
                [none, none, middle, outer, start, none],
                [middle, none, none, start, none, outer],
            )[k]
            source = jnp.concatenate([d, d[:48]] + tail, axis=0)
            result = jnp.dot(weights, source, preferred_element_type=jnp.float32)
            base = mean[o : o + 1, :] + result[members : members + 1]
            out32[pl.ds(o, members, stride=blocks), :] = result[:members] + base
    out[...] = out32[...].reshape(members, blocks, LANES).astype(jnp.bfloat16)


def apply_weights(pieces, dev, mean):
    blocks, members, cells = dev.shape
    step = 16
    f32 = jnp.float32
    return pl.pallas_call(
        apply_body,
        grid=(blocks // step,),
        out_shape=jax.ShapeDtypeStruct((members, blocks, cells), jnp.bfloat16),
        in_specs=[
            pl.BlockSpec((16, step, LANES), lambda i: (0, i, 0)),
            pl.BlockSpec((16, step, LANES), lambda i: (0, blocks // step + i, 0)),
            pl.BlockSpec((step, members, cells), lambda i: (i, 0, 0)),
            pl.BlockSpec((step, cells), lambda i: (i, 0)),
        ],
        out_specs=pl.BlockSpec((members, step, cells), lambda i: (0, i, 0)),
        scratch_shapes=[
            pltpu.VMEM((16 * step, LANES), f32),
            pltpu.VMEM((16 * step, LANES), f32),
            pltpu.VMEM((members * step, LANES), f32),
        ],
        name="apply",
    )(pieces, pieces, dev, mean)


def shards(
    obs_pert,
    innovation,
    obs_prec,
    obs_lists,
    loc_weight,
    send_rows,
    ocean_src,
    ocean_frac,
    ocean_ens,
):
    n_member = lax.axis_size("member")
    n_space = lax.axis_size("space")
    member_idx = lax.axis_index("member")
    own_members, tile_obs = obs_pert.shape
    members = own_members * n_member
    chunks = tile_obs // LANES
    b16 = jnp.bfloat16

    flat = obs_pert.reshape(own_members * chunks, LANES)
    spread = lax.all_to_all(
        jnp.broadcast_to(flat[None], (n_member, *flat.shape)), "member", 0, 0, tiled=True
    )
    spread, innovation, obs_prec, obs_lists, loc_weight, send_rows, ocean_ens = (
        lax.optimization_barrier(
            (spread, innovation, obs_prec, obs_lists, loc_weight, send_rows, ocean_ens)
        )
    )
    by_obs = spread.reshape(n_member, own_members, chunks, LANES).transpose(2, 3, 0, 1)
    by_obs = by_obs.reshape(tile_obs, members)
    own = jnp.concatenate(
        [
            by_obs,
            innovation[:, None],
            obs_prec[:, None],
            jnp.zeros((tile_obs, LANES - members - 2), b16),
        ],
        axis=1,
    )
    left = lax.ppermute(own, "space", [(i, (i + 1) % n_space) for i in range(n_space)])
    right = lax.ppermute(own, "space", [((i + 1) % n_space, i) for i in range(n_space)])

    group = obs_lists.shape[0] // n_member
    lists_mine = lax.dynamic_slice_in_dim(obs_lists, member_idx * group, group, 0)
    loc_mine = lax.dynamic_slice_in_dim(loc_weight, member_idx * group, group, 0)
    loc_mine = loc_mine.astype(jnp.float32)
    count = 2 * n_member
    home = jnp.arange(n_member, dtype=jnp.int32)[:, None] * (2 * group)
    choice = (send_rows[0] + home).T
    choice = jnp.concatenate([choice, choice + group], axis=1).reshape(-1)
    dev, mean = deviations(ocean_ens)
    lists_mine, loc_mine, left, own, right, choice, dev, mean = lax.optimization_barrier(
        (lists_mine, loc_mine, left, own, right, choice, dev, mean)
    )
    pieces = transforms(lists_mine, loc_mine, left, own, right, members)

    arrived_one = lax.all_to_all(
        pieces.reshape(n_member, 2 * group, LANES), "member", 0, 0, tiled=True
    ).reshape(n_member * 2 * group, LANES)
    arrived_one, ocean_src, ocean_frac = lax.optimization_barrier(
        (arrived_one, ocean_src, ocean_frac)
    )
    places = jnp.arange(n_member * 2 * group, dtype=jnp.int32)[None]
    pick = (choice[:, None] == places).astype(b16)
    chosen = jnp.dot(pick, arrived_one, preferred_element_type=jnp.float32).astype(b16)
    arrived = lax.all_to_all(
        chosen.reshape(n_space, count, LANES), "space", 0, 0, tiled=True
    ).reshape(n_space * count, LANES)
    slot = (ocean_src % n_space) * count + ocean_src // n_space
    slot = jnp.concatenate([slot, slot + n_member], axis=0)
    frac = jnp.concatenate([ocean_frac, ocean_frac])[:, None]
    places = jnp.arange(n_space * count, dtype=jnp.int32)[None]
    coef = jnp.where(slot[:, :1] == places, 1.0 - frac, 0.0) + jnp.where(
        slot[:, 1:] == places, frac, 0.0
    )
    halves = jnp.dot(
        coef, arrived.astype(jnp.float32), precision=lax.Precision.HIGHEST
    ).astype(b16)
    everything = lax.all_gather(halves, "member", axis=0, tiled=True)
    return apply_weights(everything.reshape(n_member, *halves.shape), dev, mean)


def solution(mesh):
    return jax.shard_map(
        shards,
        mesh=mesh,
        in_specs=(
            P("member", "space"),
            P("space"),
            P("space"),
            P("space", None),
            P("space", None),
            P("space", None, None),
            P("space", None),
            P("space"),
            P(None, "space", "member"),
        ),
        out_specs=P(None, "space", "member"),
        check_vma=False,
    )
```

time: 164 us -> 156 us (0.951)
  blocking collectives: 35.3 us -> 56.2 us
  waiting for transfers between devices: 46.5 us -> 30.6 us
  starting transfers between devices: 35.6 us -> 26.8 us
  Pallas kernels: 36.3 us -> 33.2 us
  local copies, waits for them, and re-layouts: 6.55 us -> 3.72 us
    all_to_all x0 -> x1, blocking collectives: none -> 21.7 us  [shards(): lax.all_to_all(pieces.reshape(n_member, 2 * group, LANES), 'member', 0, 0...]
    all_to_all x2 -> x1, waiting for transfers between devices: 19.7 us -> 6.75 us  [shards(): lax.all_to_all(chosen.reshape(n_space, count, LANES), 'space', 0, 0, tile...]
    all_to_all x2 -> x1, starting transfers between devices: 16 us -> 7.23 us  [shards(): lax.all_to_all(chosen.reshape(n_space, count, LANES), 'space', 0, 0, tile...]
    ppermute x1, waiting for transfers between devices: 5.93 us -> 3.03 us  [shards(): lax.ppermute(own, 'space', [(i, (i + 1) % n_space) for i in range(n_space)])]
    pallas_call x1 -> x2, Pallas kernels: 27.8 us -> 24.9 us  [the longest x1 19.4 us: transforms(): pl.pallas_call(transform_body, out_shape=jax.ShapeDtypeStruct((HALF * 2 *...]
    ppermute x1, waiting for transfers between devices: 2.13 us -> 0.01 us  [shards(): lax.ppermute(own, 'space', [((i + 1) % n_space, i) for i in range(n_space)])]
    all_to_all x1, waiting for transfers between devices: 18.7 us -> 20.8 us  [shards(): lax.all_to_all(jnp.broadcast_to(flat[None], (n_member, *flat.shape)), 'me...]
  transfers between devices with their start and end apart: 5 -> 4, of which waited for: 5 -> 3; matrix products, arithmetic and copies ran while one was open for 3% -> 1% of each run, Pallas kernels for 0% -> 4%
where the time goes in v2:
time: 156 us; the launch traced here: 155 us
  blocking collectives  56.2 us (36%)
  Pallas kernels  33.2 us (21%)
  waiting for transfers between devices  30.6 us (20%)
  starting transfers between devices  26.8 us (17%)
  local copies, waits for them, and re-layouts  3.72 us (2%)
  other arithmetic  2.09 us (1%)
  matrix products  1.84 us (1%)
    all_gather x1, blocking collectives, shards(): everything = lax.all_gather(halves, 'member', axis=0, tiled=True)  34.6 us
    all_to_all x1, blocking collectives, shards(): lax.all_to_all(pieces.reshape(n_member, 2 * group, LANES), 'member', 0, 0...  21.7 us
    all_to_all x1, waiting for transfers between devices, shards(): lax.all_to_all(jnp.broadcast_to(flat[None], (n_member, *flat.shape)), 'me...  20.8 us
    pallas_call x1, Pallas kernels, transforms(): pl.pallas_call(transform_body, out_shape=jax.ShapeDtypeStruct((HALF * 2 *...  19.4 us
    all_to_all x1, starting transfers between devices, shards(): lax.all_to_all(jnp.broadcast_to(flat[None], (n_member, *flat.shape)), 'me...  15.2 us
    pallas_call x1, Pallas kernels, apply_weights(): pl.pallas_call(apply_body, grid=(blocks // step,), out_shape=jax.ShapeDty...  8.22 us
    all_to_all x1, starting transfers between devices, shards(): lax.all_to_all(chosen.reshape(n_space, count, LANES), 'space', 0, 0, tile...  7.23 us
    all_to_all x1, waiting for transfers between devices, shards(): lax.all_to_all(chosen.reshape(n_space, count, LANES), 'space', 0, 0, tile...  6.75 us
  transfers between devices with their start and end apart: 4, of which 3 were waited for; matrix products, arithmetic and copies ran while one was open for 1% of the time, Pallas kernels for 4%

profile of v2, /device:TPU:6, one launch (start us, length us, event | category | flops | bytes accessed | tf_op | source)
XLA Modules:
  0.0 154.5 jit_solution(9832512196486521223)
XLA Ops:
  0.0 0.9 broadcast_in_dim.39
  0.9 0.8 broadcast_in_dim.40
  1.6 15.2 %all-to-all-start = ((bf16[16,80,128]{2,1,0:T(8,128)(2,1)}), bf16[16,80,128]{2,1,0:T(8,128)(2,1)S(1)}, u32[]{:S(2)}, u32[]{:S(2)}) async-start(bf16[16,80,128]{2,1,0:T(8,128)(2,1)} %broadcast_in_dim.40), calls=%async_computation | async-start | bytes 655360 | tf_op jit(solution)/shard_map/all_to_all | solution.py:304
  16.9 0.1 pad.9.clone
  16.9 20.8 %all-to-all-done = bf16[16,80,128]{2,1,0:T(8,128)(2,1)S(1)} async-done(((bf16[16,80,128]{2,1,0:T(8,128)(2,1)}), bf16[16,80,128]{2,1,0:T(8,128)(2,1)S(1)}, u32[]{:S(2)}, u32[]{:S(2)}) %all-to-all-start) | async-done | bytes 327712 | tf_op jit(solution)/shard_map/all_to_all | solution.py:304
  37.7 0.1 copy.16
  37.8 0.0 copy-start.4
  37.8 0.3 copy.10
  38.1 0.3 broadcast_in_dim.47
  38.5 0.3 broadcast_in_dim.48
  38.8 0.5 maximum_maximum_fusion.own
  39.3 1.9 %collective-permute-start.1 = (bf16[2048,128]{1,0:T(8,128)(2,1)S(1)}, bf16[2048,128]{1,0:T(8,128)(2,1)S(1)}, u32[]{:S(2)}, u32[]{:S(2)}) collective-permute-start(bf16[2048,128]{1,0:T(8,128)(2,1)S(1)} %maximum_maximum_fusion.own), channel_id=1, source_target_pairs={{16,0},{32,16},{48,32},{64,48},{80,64},{96,80},{112,96},{128,112},... | collective-permute-start | bytes 1572872 | tf_op jit(solution)/shard_map/ppermute | solution.py:324
  41.3 2.4 %collective-permute-start = (bf16[2048,128]{1,0:T(8,128)(2,1)S(1)}, bf16[2048,128]{1,0:T(8,128)(2,1)S(1)}, u32[]{:S(2)}, u32[]{:S(2)}) collective-permute-start(bf16[2048,128]{1,0:T(8,128)(2,1)S(1)} %maximum_maximum_fusion.own), channel_id=1, source_target_pairs={{0,16},{16,32},{32,48},{48,64},{64,80},{80,96},{96,112},{112,128},... | collective-permute-start | bytes 1572872 | tf_op jit(solution)/shard_map/ppermute | solution.py:323
  43.7 0.1 broadcast_add_fusion
  43.8 0.1 copy.13
  43.8 0.1 reshape.53
  43.9 5.6 %deviations.1 = (bf16[96,80,128]{2,1,0:T(8,128)(2,1)}, f32[96,128]{1,0:T(8,128)}) custom-call(bf16[80,96,128]{2,1,0:T(8,128)(2,1)} %ens), custom_call_target="tpu_custom_call" | custom-call | tf_op jit(solution)/shard_map/deviations/pallas_call | solution.py:174
  49.5 0.0 copy-start.8
  49.5 1.3 dynamic-slice_convert_fusion.loc
  50.8 3.0 %collective-permute-done.left = bf16[2048,128]{1,0:T(8,128)(2,1)S(1)} collective-permute-done((bf16[2048,128]{1,0:T(8,128)(2,1)S(1)}, bf16[2048,128]{1,0:T(8,128)(2,1)S(1)}, u32[]{:S(2)}, u32[]{:S(2)}) %collective-permute-start) | collective-permute-done | bytes 524320 | tf_op jit(solution)/shard_map/ppermute | solution.py:323
  53.9 0.6 reshape.54.lists
  54.5 0.2 copy-done.3
  54.7 19.4 %transforms.1 = bf16[384,128]{1,0:T(8,128)(2,1)} custom-call(s32[3072]{0:T(1024)} %reshape.54.lists, f32[12,256]{1,0:T(8,128)} %dynamic-slice_convert_fusion.loc, bf16[2048,128]{1,0:T(8,128)(2,1)} %copy-done.3, bf16[2048,128]{1,0:T(8,128)(2,1)} %copy-done.1, bf16[2048,128]{1,0:T(8,128)(2,1)} %copy-done.2), custom_call_target="tpu_custom_call" | custom-call | tf_op jit(solution)/shard_map/transforms/pallas_call | solution.py:140
  74.1 21.7 %all_to_all.15 = bf16[16,24,128]{2,1,0:T(8,128)(2,1)S(1)} all-to-all(bf16[16,24,128]{2,1,0:T(8,128)(2,1)} %bitcast.31), channel_id=1, replica_groups=mesh['space'=32,'member'=16] {'member'}, dimensions={0} | all-to-all | bytes 196608 | tf_op jit(solution)/shard_map/all_to_all | solution.py:340
  95.7 1.1 fusion.1
  96.9 7.2 %all-to-all-start.2 = ((bf16[32,32,128]{2,1,0:T(8,128)(2,1)}), bf16[32,32,128]{2,1,0:T(8,128)(2,1)S(1)}, u32[]{:S(2)}, u32[]{:S(2)}) async-start(bf16[32,32,128]{2,1,0:T(8,128)(2,1)} %bitcast.8), calls=%async_computation.2 | async-start | bytes 524288 | tf_op jit(solution)/shard_map/all_to_all | solution.py:349
  104.1 0.1 broadcast_subtract_fusion
  104.2 0.1 fusion.14
  104.3 6.7 %all-to-all-done.2 = bf16[32,32,128]{2,1,0:T(8,128)(2,1)S(1)} async-done(((bf16[32,32,128]{2,1,0:T(8,128)(2,1)}), bf16[32,32,128]{2,1,0:T(8,128)(2,1)S(1)}, u32[]{:S(2)}, u32[]{:S(2)}) %all-to-all-start.2) | async-done | bytes 262176 | tf_op jit(solution)/shard_map/all_to_all | solution.py:349
  111.0 0.7 convolution_convert_fusion
  111.7 34.6 %all_gather.3 = bf16[3072,128]{1,0:T(8,128)(2,1)} all-gather(bf16[192,128]{1,0:T(8,128)(2,1)S(1)} %convolution_convert_fusion), channel_id=1, replica_groups=mesh['space'=32,'member'=16] {'member'}, dimensions={0}, use_global_device_ids=true | all-gather | bytes 835584 | tf_op jit(solution)/shard_map/all_gather | solution.py:362
  146.3 8.2 %apply.1 = bf16[80,96,128]{2,1,0:T(8,128)(2,1)} custom-call(bf16[16,192,128]{2,1,0:T(8,128)(2,1)} %bitcast.27, bf16[16,192,128]{2,1,0:T(8,128)(2,1)} %bitcast.28, bf16[96,80,128]{2,1,0:T(8,128)(2,1)} %get-tuple-element.43.dev, f32[96,128]{1,0:T(8,128)} %get-tuple-element.44.mean), custom_call_target="tpu_custom_call" | custom-call | tf_op jit(solution)/shard_map/apply/pallas_call | solution.py:264
  (21 shorter events, 0.1 us)
Async XLA Ops:
  0.0 49.5 %copy-start = (s32[192,256]{1,0:T(8,128)S(1)}, s32[192,256]{1,0:T(8,128)}, u32[]{:S(2)}) copy-start(s32[192,256]{1,0:T(8,128)} %param.12) | copy-start | bytes 589828
  0.0 38.4 %copy-start.6 = (bf16[2048]{0:T(1024)(128)(2,1)S(1)}, bf16[2048]{0:T(1024)(128)(2,1)}, u32[]{:S(2)}) copy-start(bf16[2048]{0:T(1024)(128)(2,1)} %param.11) | copy-start | bytes 12292
  0.0 38.1 %copy-start.5 = (bf16[2048]{0:T(1024)(128)(2,1)S(1)}, bf16[2048]{0:T(1024)(128)(2,1)}, u32[]{:S(2)}) copy-start(bf16[2048]{0:T(1024)(128)(2,1)} %param.10) | copy-start | bytes 12292
  1.6 36.1 %all-to-all-start = ((bf16[16,80,128]{2,1,0:T(8,128)(2,1)}), bf16[16,80,128]{2,1,0:T(8,128)(2,1)S(1)}, u32[]{:S(2)}, u32[]{:S(2)}) async-start(bf16[16,80,128]{2,1,0:T(8,128)(2,1)} %broadcast_in_dim.40), calls=%async_computation | async-start | bytes 655360 | tf_op jit(solution)/shard_map/all_to_all | solution.py:304
  37.8 5.9 %copy-start.4 = (s32[1,16,32]{2,1,0:T(8,128)S(1)}, s32[1,16,32]{2,1,0:T(8,128)}, u32[]{:S(2)}) copy-start(s32[1,16,32]{2,1,0:T(8,128)} %param.14) | copy-start | bytes 6148
  39.3 15.2 %copy-start.1 = (bf16[2048,128]{1,0:T(8,128)(2,1)}, bf16[2048,128]{1,0:T(8,128)(2,1)S(1)}, u32[]{:S(2)}) copy-start(bf16[2048,128]{1,0:T(8,128)(2,1)S(1)} %maximum_maximum_fusion.own) | copy-start | bytes 1572868
  39.3 11.5 %collective-permute-start.1 = (bf16[2048,128]{1,0:T(8,128)(2,1)S(1)}, bf16[2048,128]{1,0:T(8,128)(2,1)S(1)}, u32[]{:S(2)}, u32[]{:S(2)}) collective-permute-start(bf16[2048,128]{1,0:T(8,128)(2,1)S(1)} %maximum_maximum_fusion.own), channel_id=1, source_target_pairs={{16,0},{32,16},{48,32},{64,48},{80,64},{96,80},{112,96},{128,112},... | collective-permute-start | bytes 1572872 | tf_op jit(solution)/shard_map/ppermute | solution.py:324
  41.3 12.6 %collective-permute-start = (bf16[2048,128]{1,0:T(8,128)(2,1)S(1)}, bf16[2048,128]{1,0:T(8,128)(2,1)S(1)}, u32[]{:S(2)}, u32[]{:S(2)}) collective-permute-start(bf16[2048,128]{1,0:T(8,128)(2,1)S(1)} %maximum_maximum_fusion.own), channel_id=1, source_target_pairs={{0,16},{16,32},{32,48},{48,64},{64,80},{80,96},{96,112},{112,128},... | collective-permute-start | bytes 1572872 | tf_op jit(solution)/shard_map/ppermute | solution.py:323
  49.5 54.6 %copy-start.7 = (s32[96,2]{0,1:T(2,128)S(1)}, s32[96,2]{0,1:T(2,128)}, u32[]{:S(2)}) copy-start(s32[96,2]{0,1:T(2,128)} %param.15) | copy-start | bytes 2308
  49.5 54.7 %copy-start.8 = (f32[96]{0:T(128)S(1)}, f32[96]{0:T(128)}, u32[]{:S(2)}) copy-start(f32[96]{0:T(128)} %param.16) | copy-start | bytes 1156
  50.8 3.7 %copy-start.2 = (bf16[2048,128]{1,0:T(8,128)(2,1)}, bf16[2048,128]{1,0:T(8,128)(2,1)S(1)}, u32[]{:S(2)}) copy-start(bf16[2048,128]{1,0:T(8,128)(2,1)S(1)} %collective-permute-done.1.right) | copy-start | bytes 1572868
  53.9 0.8 copy-start.3
  96.9 14.2 %all-to-all-start.2 = ((bf16[32,32,128]{2,1,0:T(8,128)(2,1)}), bf16[32,32,128]{2,1,0:T(8,128)(2,1)S(1)}, u32[]{:S(2)}, u32[]{:S(2)}) async-start(bf16[32,32,128]{2,1,0:T(8,128)(2,1)} %bitcast.8), calls=%async_computation.2 | async-start | bytes 524288 | tf_op jit(solution)/shard_map/all_to_all | solution.py:349

commit v3 on v2

--- a/solution.py
+++ b/solution.py
@@ -8,6 +8,10 @@
 ITERS = 12
 LANES = 128
 HALF = 16
+
+
+def in_vmem(x):
+    return pltpu.with_memory_space_constraint(x, pltpu.VMEM)
 
 
 def iota2(shape, dim):
@@ -64,7 +68,7 @@
         for k in range(batch):
             a = i * batch + k
             y = rows[pl.ds(a * local, local), :]
-            turned = jnp.transpose(y)[:88]
+            turned = jnp.transpose(y.astype(jnp.bfloat16))[:96].astype(jnp.float32)
             weight = loc[pl.ds(a, 1), :] * turned[members + 1 : members + 2]
             high, low = split(turned * weight)
             y16 = y.astype(jnp.bfloat16)
@@ -139,7 +143,7 @@
     stacked = pltpu.VMEM((group, 2 * LANES, LANES), b16)
     return pl.pallas_call(
         transform_body,
-        out_shape=jax.ShapeDtypeStruct((HALF * 2 * group, LANES), b16),
+        out_shape=pltpu.VMEM((HALF * 2 * group, LANES), b16),
         in_specs=[pl.BlockSpec(memory_space=pltpu.SMEM), vmem, vmem, vmem, vmem],
         out_specs=vmem,
         scratch_shapes=[
@@ -155,43 +159,47 @@
             pltpu.VMEM((HALF * 2 * group, LANES), f32),
         ],
         name="transforms",
-    )(lists, loc, left, own, right)
+    )(lists, in_vmem(loc), in_vmem(left), in_vmem(own), in_vmem(right))
 
 
 def deviation_body(ens, dev, mean, ens32):
-    members, blocks = ens.shape[0], ens.shape[1]
+    members, step = ens.shape[0], ens.shape[1]
     wide = ens[...].astype(jnp.float32)
     center = jnp.sum(wide, axis=0) * (1.0 / members)
-    mean[...] = center
-    ens32[...] = (wide - center[None]).reshape(members * blocks, LANES)
-    for o in range(blocks):
-        dev[o] = ens32[pl.ds(o, members, stride=blocks), :].astype(jnp.bfloat16)
+    first = pl.program_id(0) * step
+    mean[pl.ds(pl.multiple_of(first, step), step), :] = center
+    ens32[...] = (wide - center[None]).reshape(members * step, LANES)
+    for o in range(step):
+        dev[first + o] = ens32[pl.ds(o, members, stride=step), :].astype(jnp.bfloat16)
 
 
 def deviations(ensemble):
     members, blocks, cells = ensemble.shape
-    step = 16
+    step = 48
+    whole = pl.BlockSpec(memory_space=pltpu.VMEM)
     return pl.pallas_call(
         deviation_body,
         grid=(blocks // step,),
         out_shape=(
-            jax.ShapeDtypeStruct((blocks, members, cells), jnp.bfloat16),
-            jax.ShapeDtypeStruct((blocks, cells), jnp.float32),
+            pltpu.VMEM((blocks, members, cells), jnp.bfloat16),
+            pltpu.VMEM((blocks, cells), jnp.float32),
         ),
         in_specs=[pl.BlockSpec((members, step, cells), lambda i: (0, i, 0))],
-        out_specs=(
-            pl.BlockSpec((step, members, cells), lambda i: (i, 0, 0)),
-            pl.BlockSpec((step, cells), lambda i: (i, 0)),
-        ),
+        out_specs=(whole, whole),
         scratch_shapes=[pltpu.VMEM((members * step, LANES), jnp.float32)],
         name="deviations",
     )(ensemble)
 
 
-def apply_body(pieces, pieces2, dev, mean, out, mix32, mix32b, out32):
+def apply_body(pieces, dev, mean, out, mix32, mix32b, out32):
     members, blocks = out.shape[0], out.shape[1]
-    mix32[...] = pieces[...].astype(jnp.float32).reshape(16 * blocks, LANES)
-    mix32b[...] = pieces2[...].astype(jnp.float32).reshape(16 * blocks, LANES)
+    begin = pl.program_id(0) * blocks
+    begin = pl.multiple_of(begin, blocks)
+    other = pl.multiple_of(begin + dev.shape[0], blocks)
+    for ref, at in ((mix32, begin), (mix32b, other)):
+        part = pieces[:, pl.ds(at, blocks), :]
+        ref[...] = part.astype(jnp.float32).reshape(16 * blocks, LANES)
+    centers = mean[pl.ds(begin, blocks), :]
     lane = iota2((16, LANES), 1)
     row = iota2((16, LANES), 0)
     lane8, row8 = lane[:8], row[:8]
@@ -242,7 +250,7 @@
                 ],
                 axis=1,
             )
-            d = dev[o]
+            d = dev[begin + o]
             outer, middle, start = d[48:80], d[16:48], d[0:16]
             tail = (
                 [outer, middle, start, none, none, none],
@@ -252,25 +260,20 @@
             )[k]
             source = jnp.concatenate([d, d[:48]] + tail, axis=0)
             result = jnp.dot(weights, source, preferred_element_type=jnp.float32)
-            base = mean[o : o + 1, :] + result[members : members + 1]
+            base = centers[o : o + 1, :] + result[members : members + 1]
             out32[pl.ds(o, members, stride=blocks), :] = result[:members] + base
     out[...] = out32[...].reshape(members, blocks, LANES).astype(jnp.bfloat16)
 
 
 def apply_weights(pieces, dev, mean):
     blocks, members, cells = dev.shape
-    step = 16
+    step = 48
     f32 = jnp.float32
     return pl.pallas_call(
         apply_body,
         grid=(blocks // step,),
         out_shape=jax.ShapeDtypeStruct((members, blocks, cells), jnp.bfloat16),
-        in_specs=[
-            pl.BlockSpec((16, step, LANES), lambda i: (0, i, 0)),
-            pl.BlockSpec((16, step, LANES), lambda i: (0, blocks // step + i, 0)),
-            pl.BlockSpec((step, members, cells), lambda i: (i, 0, 0)),
-            pl.BlockSpec((step, cells), lambda i: (i, 0)),
-        ],
+        in_specs=[pl.BlockSpec(memory_space=pltpu.VMEM)] * 3,
         out_specs=pl.BlockSpec((members, step, cells), lambda i: (0, i, 0)),
         scratch_shapes=[
             pltpu.VMEM((16 * step, LANES), f32),
@@ -278,7 +281,7 @@
             pltpu.VMEM((members * step, LANES), f32),
         ],
         name="apply",
-    )(pieces, pieces, dev, mean)
+    )(in_vmem(pieces), in_vmem(dev), in_vmem(mean))
 
 
 def shards(

time: 156 us -> 150 us (0.962)
  Pallas kernels: 33.2 us -> 27.4 us
  blocking collectives: 56.2 us -> 54 us
  waiting for transfers between devices: 30.6 us -> 32.5 us
    pallas_call x2, Pallas kernels: 24.9 us -> 21.2 us  [the longest x1 18.1 us: transforms(): pl.pallas_call(transform_body, out_shape=pltpu.VMEM((HALF * 2 * group, LA...]
    all_gather x1, blocking collectives: 34.6 us -> 32.4 us  [shards(): everything = lax.all_gather(halves, 'member', axis=0, tiled=True)]
    pallas_call x1, Pallas kernels: 8.22 us -> 6.21 us  [apply_weights(): pl.pallas_call(apply_body, grid=(blocks // step,), out_shape=jax.ShapeDty...]
    ppermute x1, waiting for transfers between devices: 3.03 us -> 4.99 us  [shards(): lax.ppermute(own, 'space', [(i, (i + 1) % n_space) for i in range(n_space)])]
  transfers between devices with their start and end apart: 4 -> 4, of which waited for: 3 -> 3; matrix products, arithmetic and copies ran while one was open for 1% -> 1% of each run, Pallas kernels for 4% -> 2%
where the time goes in v3:
time: 150 us; the launch traced here: 149 us
  blocking collectives  54 us (36%)
  waiting for transfers between devices  32.5 us (22%)
  Pallas kernels  27.4 us (18%)
  starting transfers between devices  26.8 us (18%)
  local copies, waits for them, and re-layouts  4.79 us (3%)
  matrix products  1.84 us (1%)
    all_gather x1, blocking collectives, shards(): everything = lax.all_gather(halves, 'member', axis=0, tiled=True)  32.4 us
    all_to_all x1, blocking collectives, shards(): lax.all_to_all(pieces.reshape(n_member, 2 * group, LANES), 'member', 0, 0...  21.6 us
    all_to_all x1, waiting for transfers between devices, shards(): lax.all_to_all(jnp.broadcast_to(flat[None], (n_member, *flat.shape)), 'me...  20.8 us
    pallas_call x1, Pallas kernels, transforms(): pl.pallas_call(transform_body, out_shape=pltpu.VMEM((HALF * 2 * group, LA...  18.1 us
    all_to_all x1, starting transfers between devices, shards(): lax.all_to_all(jnp.broadcast_to(flat[None], (n_member, *flat.shape)), 'me...  15.2 us
    all_to_all x1, starting transfers between devices, shards(): lax.all_to_all(chosen.reshape(n_space, count, LANES), 'space', 0, 0, tile...  7.29 us
    all_to_all x1, waiting for transfers between devices, shards(): lax.all_to_all(chosen.reshape(n_space, count, LANES), 'space', 0, 0, tile...  6.75 us
    pallas_call x1, Pallas kernels, apply_weights(): pl.pallas_call(apply_body, grid=(blocks // step,), out_shape=jax.ShapeDty...  6.21 us
  transfers between devices with their start and end apart: 4, of which 3 were waited for; matrix products, arithmetic and copies ran while one was open for 1% of the time, Pallas kernels for 2%

profile of v3, /device:TPU:6, one launch (start us, length us, event | category | flops | bytes accessed | tf_op | source)
XLA Modules:
  0.0 149.1 jit_solution(14054191849885688023)
XLA Ops:
  0.0 0.9 broadcast_in_dim.39
  0.9 0.8 broadcast_in_dim.40
  1.6 15.2 %all-to-all-start = ((bf16[16,80,128]{2,1,0:T(8,128)(2,1)}), bf16[16,80,128]{2,1,0:T(8,128)(2,1)S(1)}, u32[]{:S(2)}, u32[]{:S(2)}) async-start(bf16[16,80,128]{2,1,0:T(8,128)(2,1)} %broadcast_in_dim.40), calls=%async_computation | async-start | bytes 655360 | tf_op jit(solution)/shard_map/all_to_all | solution.py:307
  16.9 0.1 pad.9.clone
  16.9 20.8 %all-to-all-done = bf16[16,80,128]{2,1,0:T(8,128)(2,1)S(1)} async-done(((bf16[16,80,128]{2,1,0:T(8,128)(2,1)}), bf16[16,80,128]{2,1,0:T(8,128)(2,1)S(1)}, u32[]{:S(2)}, u32[]{:S(2)}) %all-to-all-start) | async-done | bytes 327712 | tf_op jit(solution)/shard_map/all_to_all | solution.py:307
  37.7 0.1 copy.16
  37.8 0.0 copy-start.3
  37.8 0.3 copy.10
  38.1 0.3 broadcast_in_dim.47
  38.5 0.3 broadcast_in_dim.48
  38.8 0.5 maximum_maximum_fusion.own
  39.3 1.9 %collective-permute-start.1 = (bf16[2048,128]{1,0:T(8,128)(2,1)S(1)}, bf16[2048,128]{1,0:T(8,128)(2,1)S(1)}, u32[]{:S(2)}, u32[]{:S(2)}) collective-permute-start(bf16[2048,128]{1,0:T(8,128)(2,1)S(1)} %maximum_maximum_fusion.own), channel_id=1, source_target_pairs={{16,0},{32,16},{48,32},{64,48},{80,64},{96,80},{112,96},{128,112},... | collective-permute-start | bytes 1572872 | tf_op jit(solution)/shard_map/ppermute | solution.py:327
  41.2 2.4 %collective-permute-start = (bf16[2048,128]{1,0:T(8,128)(2,1)S(1)}, bf16[2048,128]{1,0:T(8,128)(2,1)}, u32[]{:S(2)}, u32[]{:S(2)}) collective-permute-start(bf16[2048,128]{1,0:T(8,128)(2,1)S(1)} %maximum_maximum_fusion.own), channel_id=1, source_target_pairs={{0,16},{16,32},{32,48},{48,64},{64,80},{80,96},{96,112},{112,128},... | collective-permute-start | bytes 1572872 | tf_op jit(solution)/shard_map/ppermute | solution.py:326
  43.7 0.1 broadcast_add_fusion
  43.7 0.1 copy.13
  43.8 0.1 reshape.53
  43.9 3.0 %deviations.1 = (bf16[96,80,128]{2,1,0:T(8,128)(2,1)S(1)}, f32[96,128]{1,0:T(8,128)S(1)}) custom-call(bf16[80,96,128]{2,1,0:T(8,128)(2,1)} %ens), custom_call_target="tpu_custom_call" | custom-call | tf_op jit(solution)/shard_map/deviations/pallas_call | solution.py:180
  47.0 1.3 copy-done.1
  48.2 0.7 dynamic-slice_convert_fusion.loc
  49.0 5.0 %collective-permute-done.left = bf16[2048,128]{1,0:T(8,128)(2,1)} collective-permute-done((bf16[2048,128]{1,0:T(8,128)(2,1)S(1)}, bf16[2048,128]{1,0:T(8,128)(2,1)}, u32[]{:S(2)}, u32[]{:S(2)}) %collective-permute-start) | collective-permute-done | bytes 524320 | tf_op jit(solution)/shard_map/ppermute | solution.py:326
  54.0 0.6 reshape.54.lists
  54.6 18.1 %transforms.1 = bf16[384,128]{1,0:T(8,128)(2,1)S(1)} custom-call(s32[3072]{0:T(1024)} %reshape.54.lists, f32[12,256]{1,0:T(8,128)S(1)} %dynamic-slice_convert_fusion.loc, bf16[2048,128]{1,0:T(8,128)(2,1)} %collective-permute-done.left, bf16[2048,128]{1,0:T(8,128)(2,1)S(1)} %maximum_maximum_fusion.own, bf16[2048,128]{1,0:T(8,128)(2,1)S(1)} %collective-permute-done.1.right), custom_call_target="tpu_custom_call" | custom-call | tf_op jit(solution)/shard_map/transforms/pallas_call | solution.py:144
  72.7 0.0 copy-start.2
  72.7 21.6 %all_to_all.15 = bf16[16,24,128]{2,1,0:T(8,128)(2,1)S(1)} all-to-all(bf16[16,24,128]{2,1,0:T(8,128)(2,1)S(1)} %bitcast.28), channel_id=1, replica_groups=mesh['space'=32,'member'=16] {'member'}, dimensions={0} | all-to-all | bytes 196608 | tf_op jit(solution)/shard_map/all_to_all | solution.py:343
  94.3 1.1 fusion.1
  95.5 7.3 %all-to-all-start.2 = ((bf16[32,32,128]{2,1,0:T(8,128)(2,1)}), bf16[32,32,128]{2,1,0:T(8,128)(2,1)S(1)}, u32[]{:S(2)}, u32[]{:S(2)}) async-start(bf16[32,32,128]{2,1,0:T(8,128)(2,1)} %bitcast.8), calls=%async_computation.2 | async-start | bytes 524288 | tf_op jit(solution)/shard_map/all_to_all | solution.py:352
  102.8 0.1 broadcast_subtract_fusion
  102.9 0.1 fusion.14
  103.0 6.7 %all-to-all-done.2 = bf16[32,32,128]{2,1,0:T(8,128)(2,1)S(1)} async-done(((bf16[32,32,128]{2,1,0:T(8,128)(2,1)}), bf16[32,32,128]{2,1,0:T(8,128)(2,1)S(1)}, u32[]{:S(2)}, u32[]{:S(2)}) %all-to-all-start.2) | async-done | bytes 262176 | tf_op jit(solution)/shard_map/all_to_all | solution.py:352
  109.7 0.7 convolution_convert_fusion
  110.4 32.4 %all_gather.3 = bf16[3072,128]{1,0:T(8,128)(2,1)S(1)} all-gather(bf16[192,128]{1,0:T(8,128)(2,1)S(1)} %convolution_convert_fusion), channel_id=1, replica_groups=mesh['space'=32,'member'=16] {'member'}, dimensions={0}, use_global_device_ids=true | all-gather | bytes 835584 | tf_op jit(solution)/shard_map/all_gather | solution.py:365
  142.8 6.2 %apply.1 = bf16[80,96,128]{2,1,0:T(8,128)(2,1)} custom-call(bf16[16,192,128]{2,1,0:T(8,128)(2,1)S(1)} %bitcast.27, bf16[96,80,128]{2,1,0:T(8,128)(2,1)S(1)} %copy-done.2, f32[96,128]{1,0:T(8,128)S(1)} %get-tuple-element.44.mean), custom_call_target="tpu_custom_call" | custom-call | tf_op jit(solution)/shard_map/apply/pallas_call | solution.py:272
  (19 shorter events, 0.1 us)
Async XLA Ops:
  0.0 48.2 %copy-start = (s32[192,256]{1,0:T(8,128)S(1)}, s32[192,256]{1,0:T(8,128)}, u32[]{:S(2)}) copy-start(s32[192,256]{1,0:T(8,128)} %param.12) | copy-start | bytes 589828
  0.0 38.4 %copy-start.5 = (bf16[2048]{0:T(1024)(128)(2,1)S(1)}, bf16[2048]{0:T(1024)(128)(2,1)}, u32[]{:S(2)}) copy-start(bf16[2048]{0:T(1024)(128)(2,1)} %param.11) | copy-start | bytes 12292
  0.0 38.1 %copy-start.4 = (bf16[2048]{0:T(1024)(128)(2,1)S(1)}, bf16[2048]{0:T(1024)(128)(2,1)}, u32[]{:S(2)}) copy-start(bf16[2048]{0:T(1024)(128)(2,1)} %param.10) | copy-start | bytes 12292
  1.6 36.1 %all-to-all-start = ((bf16[16,80,128]{2,1,0:T(8,128)(2,1)}), bf16[16,80,128]{2,1,0:T(8,128)(2,1)S(1)}, u32[]{:S(2)}, u32[]{:S(2)}) async-start(bf16[16,80,128]{2,1,0:T(8,128)(2,1)} %broadcast_in_dim.40), calls=%async_computation | async-start | bytes 655360 | tf_op jit(solution)/shard_map/all_to_all | solution.py:307
  37.8 5.9 %copy-start.3 = (s32[1,16,32]{2,1,0:T(8,128)S(1)}, s32[1,16,32]{2,1,0:T(8,128)}, u32[]{:S(2)}) copy-start(s32[1,16,32]{2,1,0:T(8,128)} %param.14) | copy-start | bytes 6148
  39.3 9.7 %collective-permute-start.1 = (bf16[2048,128]{1,0:T(8,128)(2,1)S(1)}, bf16[2048,128]{1,0:T(8,128)(2,1)S(1)}, u32[]{:S(2)}, u32[]{:S(2)}) collective-permute-start(bf16[2048,128]{1,0:T(8,128)(2,1)S(1)} %maximum_maximum_fusion.own), channel_id=1, source_target_pairs={{16,0},{32,16},{48,32},{64,48},{80,64},{96,80},{112,96},{128,112},... | collective-permute-start | bytes 1572872 | tf_op jit(solution)/shard_map/ppermute | solution.py:327
  41.2 12.7 %collective-permute-start = (bf16[2048,128]{1,0:T(8,128)(2,1)S(1)}, bf16[2048,128]{1,0:T(8,128)(2,1)}, u32[]{:S(2)}, u32[]{:S(2)}) collective-permute-start(bf16[2048,128]{1,0:T(8,128)(2,1)S(1)} %maximum_maximum_fusion.own), channel_id=1, source_target_pairs={{0,16},{16,32},{32,48},{48,64},{64,80},{80,96},{96,112},{112,128},... | collective-permute-start | bytes 1572872 | tf_op jit(solution)/shard_map/ppermute | solution.py:326
  46.9 1.3 copy-start.1
  48.2 54.6 %copy-start.6 = (s32[96,2]{0,1:T(2,128)S(1)}, s32[96,2]{0,1:T(2,128)}, u32[]{:S(2)}) copy-start(s32[96,2]{0,1:T(2,128)} %param.15) | copy-start | bytes 2308
  48.2 54.6 %copy-start.7 = (f32[96]{0:T(128)S(1)}, f32[96]{0:T(128)}, u32[]{:S(2)}) copy-start(f32[96]{0:T(128)} %param.16) | copy-start | bytes 1156
  72.7 70.1 %copy-start.2 = (bf16[96,80,128]{2,1,0:T(8,128)(2,1)S(1)}, bf16[96,80,128]{2,1,0:T(8,128)(2,1)}, u32[]{:S(2)}) copy-start(bf16[96,80,128]{2,1,0:T(8,128)(2,1)} %copy-done.1) | copy-start | bytes 5898244
  95.5 14.2 %all-to-all-start.2 = ((bf16[32,32,128]{2,1,0:T(8,128)(2,1)}), bf16[32,32,128]{2,1,0:T(8,128)(2,1)S(1)}, u32[]{:S(2)}, u32[]{:S(2)}) async-start(bf16[32,32,128]{2,1,0:T(8,128)(2,1)} %bitcast.8), calls=%async_computation.2 | async-start | bytes 524288 | tf_op jit(solution)/shard_map/all_to_all | solution.py:352

commit v4 on v3

--- a/solution.py
+++ b/solution.py
@@ -24,19 +24,23 @@
     return high, low
 
 
-def as_left(x):
-    lane = iota2(x.shape, 1)
-    high = x.astype(jnp.bfloat16).astype(jnp.float32)
-    low = pltpu.roll(x - high, 80, 1)
+def as_left(high, low):
+    lane = iota2(high.shape, 1)
+    low = pltpu.roll(low, 80, 1)
     again = pltpu.roll(high, 32, 1)
     first = jnp.where(lane < 80, high, low)
     second = jnp.where(lane < 32, low, again)
-    return jnp.concatenate([first.astype(jnp.bfloat16), second.astype(jnp.bfloat16)], axis=1)
-
-
-def as_right(x):
-    high, low = split(x)
-    return jnp.concatenate([high, high, low, jnp.zeros((16, x.shape[1]), jnp.bfloat16)], axis=0)
+    return jnp.concatenate([first, second], axis=1)
+
+
+def as_right(high, low):
+    none = jnp.zeros((16, high.shape[1]), jnp.bfloat16)
+    return jnp.concatenate([high, high, low, none], axis=0)
+
+
+def both(x):
+    parts = split(x)
+    return as_left(*parts), as_right(*parts)
 
 
 def product(left, right):
@@ -79,25 +83,19 @@
             )
             side[a, 0:1, :] = gram[members : members + 1, :]
             side[a, 1:2, :] = jnp.broadcast_to(trace, (1, LANES))
-            start = mat / trace
-            corr = 1.5 * eye - 0.5 * start
-            right = as_right(corr)
-            zl[a], zr[a] = as_left(corr), right
-            root = product(as_left(start), right)
-            rl[a], rr[a] = as_left(root), as_right(root)
+            start = mat * (0.5 / trace)
+            zl[a], zr[a] = both(1.5 * eye - start)
+            rl[a], rr[a] = both(product(as_left(*split(start)), zr[a]))
         return carry
 
     lax.fori_loop(0, group // batch, begin, 0)
 
     def newton(i, carry):
         for a in range(group):
-            corr = 1.5 * eye - 0.5 * product(zl[a], rr[a])
-            ml[a], mr[a] = as_left(corr), as_right(corr)
+            ml[a], mr[a] = both(1.5 * eye - product(zl[a], rr[a]))
         for a in range(group):
-            root = product(rl[a], mr[a])
-            inverse = product(ml[a], zr[a])
-            rl[a], rr[a] = as_left(root), as_right(root)
-            zl[a], zr[a] = as_left(inverse), as_right(inverse)
+            rl[a], rr[a] = both(product(rl[a], mr[a]))
+            zl[a], zr[a] = both(product(ml[a], zr[a]))
         return carry
 
     lax.fori_loop(0, ITERS - 2, newton, 0)
@@ -107,8 +105,8 @@
     def finish(i, carry):
         for k in range(batch):
             a = i * batch + k
-            corr = 1.5 * eye - 0.5 * product(zl[a], rr[a])
-            inverse = product(as_left(corr), zr[a])
+            corr = 1.5 * eye - product(zl[a], rr[a])
+            inverse = product(as_left(*split(corr)), zr[a])
             trace = side[a, 1:2, :]
             half_way = jnp.sum(
                 jnp.where(inside, inverse * side[a, 0:1, :], 0.0), axis=1, keepdims=True
@@ -135,7 +133,6 @@
 
 def transforms(lists, loc, left, own, right, members):
     group, local = loc.shape
-    lists = lists.reshape(-1)
     tile = own.shape[0]
     f32, b16 = jnp.float32, jnp.bfloat16
     vmem = pl.BlockSpec(memory_space=pltpu.VMEM)
@@ -160,6 +157,30 @@
         ],
         name="transforms",
     )(lists, in_vmem(loc), in_vmem(left), in_vmem(own), in_vmem(right))
+
+
+def spread_body(pert, out, flat):
+    wide = pert[...].astype(jnp.float32)
+    count, tile = wide.shape
+    for c in range(tile // LANES):
+        flat[c * count : (c + 1) * count, :] = wide[:, c * LANES : (c + 1) * LANES]
+    rows = flat[...].astype(jnp.bfloat16)
+    for p in range(out.shape[0]):
+        out[p] = rows
+
+
+def copies(pert, devices):
+    count, tile = pert.shape
+    shape = (count * tile // LANES, LANES)
+    vmem = pl.BlockSpec(memory_space=pltpu.VMEM)
+    return pl.pallas_call(
+        spread_body,
+        out_shape=pltpu.VMEM((devices, *shape), jnp.bfloat16),
+        in_specs=[vmem],
+        out_specs=vmem,
+        scratch_shapes=[pltpu.VMEM(shape, jnp.float32)],
+        name="copies",
+    )(pert)
 
 
 def deviation_body(ens, dev, mean, ens32):
@@ -303,16 +324,11 @@
     chunks = tile_obs // LANES
     b16 = jnp.bfloat16
 
-    flat = obs_pert.reshape(own_members * chunks, LANES)
-    spread = lax.all_to_all(
-        jnp.broadcast_to(flat[None], (n_member, *flat.shape)), "member", 0, 0, tiled=True
-    )
-    spread, innovation, obs_prec, obs_lists, loc_weight, send_rows, ocean_ens = (
-        lax.optimization_barrier(
-            (spread, innovation, obs_prec, obs_lists, loc_weight, send_rows, ocean_ens)
-        )
-    )
-    by_obs = spread.reshape(n_member, own_members, chunks, LANES).transpose(2, 3, 0, 1)
+    spread = lax.all_to_all(copies(obs_pert, n_member), "member", 0, 0, tiled=True)
+    spread, obs_lists, loc_weight, send_rows, ocean_ens = lax.optimization_barrier(
+        (spread, obs_lists, loc_weight, send_rows, ocean_ens)
+    )
+    by_obs = spread.reshape(n_member, chunks, own_members, LANES).transpose(1, 3, 0, 2)
     by_obs = by_obs.reshape(tile_obs, members)
     own = jnp.concatenate(
         [
@@ -327,7 +343,7 @@
     right = lax.ppermute(own, "space", [((i + 1) % n_space, i) for i in range(n_space)])
 
     group = obs_lists.shape[0] // n_member
-    lists_mine = lax.dynamic_slice_in_dim(obs_lists, member_idx * group, group, 0)
+    lists_mine = lax.dynamic_slice_in_dim(obs_lists, member_idx * group, group, 0).reshape(-1)
     loc_mine = lax.dynamic_slice_in_dim(loc_weight, member_idx * group, group, 0)
     loc_mine = loc_mine.astype(jnp.float32)
     count = 2 * n_member

time: 150 us -> 149 us (level)
  waiting for transfers between devices: 32.5 us -> 29.8 us
    all_to_all x1, waiting for transfers between devices: 20.8 us -> 18.7 us  [shards(): lax.all_to_all(copies(obs_pert, n_member), 'member', 0, 0, tiled=True)]
    broadcast_in_dim x2 -> x0, local copies, waits for them, and re-layouts: 1.63 us -> none  [shards(): jnp.broadcast_to(flat[None], (n_member, *flat.shape))]
    pallas_call x0 -> x1, Pallas kernels: none -> 1.55 us  [copies(): pl.pallas_call(spread_body, out_shape=pltpu.VMEM((devices, *shape), jnp.b...]
  transfers between devices with their start and end apart: 4 -> 4, of which waited for: 3 -> 3; matrix products, arithmetic and copies ran while one was open for 1% -> 3% of each run, Pallas kernels for 2% -> 2%
where the time goes in v4:
time: 149 us; the launch traced here: 148 us
  blocking collectives  54 us (36%)
  waiting for transfers between devices  29.8 us (20%)
  Pallas kernels  28.8 us (19%)
  starting transfers between devices  26.8 us (18%)
  local copies, waits for them, and re-layouts  4.7 us (3%)
  matrix products  1.83 us (1%)
  other arithmetic  1.51 us (1%)
    all_gather x1, blocking collectives, shards(): everything = lax.all_gather(halves, 'member', axis=0, tiled=True)  32.4 us
    all_to_all x1, blocking collectives, shards(): lax.all_to_all(pieces.reshape(n_member, 2 * group, LANES), 'member', 0, 0...  21.6 us
    all_to_all x1, waiting for transfers between devices, shards(): lax.all_to_all(copies(obs_pert, n_member), 'member', 0, 0, tiled=True)  18.7 us
    pallas_call x1, Pallas kernels, transforms(): pl.pallas_call(transform_body, out_shape=pltpu.VMEM((HALF * 2 * group, LA...  18 us
    all_to_all x1, starting transfers between devices, shards(): lax.all_to_all(copies(obs_pert, n_member), 'member', 0, 0, tiled=True)  15.2 us
    all_to_all x1, starting transfers between devices, shards(): lax.all_to_all(chosen.reshape(n_space, count, LANES), 'space', 0, 0, tile...  7.29 us
    all_to_all x1, waiting for transfers between devices, shards(): lax.all_to_all(chosen.reshape(n_space, count, LANES), 'space', 0, 0, tile...  6.75 us
    pallas_call x1, Pallas kernels, apply_weights(): pl.pallas_call(apply_body, grid=(blocks // step,), out_shape=jax.ShapeDty...  6.21 us
  transfers between devices with their start and end apart: 4, of which 3 were waited for; matrix products, arithmetic and copies ran while one was open for 3% of the time, Pallas kernels for 2%

profile of v4, /device:TPU:6, one launch (start us, length us, event | category | flops | bytes accessed | tf_op | source)
XLA Modules:
  0.0 147.7 jit_solution(17956635138391865540)
XLA Ops:
  0.0 1.6 %copies.1 = bf16[16,80,128]{2,1,0:T(8,128)(2,1)} custom-call(bf16[5,2048]{1,0:T(8,128)(2,1)} %pert.1), custom_call_target="tpu_custom_call" | custom-call | tf_op jit(solution)/shard_map/copies/pallas_call | solution.py:176
  1.6 15.2 %all-to-all-start = ((bf16[16,80,128]{2,1,0:T(8,128)(2,1)}), bf16[16,80,128]{2,1,0:T(8,128)(2,1)S(1)}, u32[]{:S(2)}, u32[]{:S(2)}) async-start(bf16[16,80,128]{2,1,0:T(8,128)(2,1)} %copies.1), calls=%async_computation | async-start | bytes 655360 | tf_op jit(solution)/shard_map/all_to_all | solution.py:327
  16.8 1.0 broadcast_in_dim.38
  17.8 1.0 broadcast_in_dim.39
  18.8 0.1 pad.9.clone
  18.9 18.7 %all-to-all-done = bf16[16,80,128]{2,1,0:T(8,128)(2,1)S(1)} async-done(((bf16[16,80,128]{2,1,0:T(8,128)(2,1)}), bf16[16,80,128]{2,1,0:T(8,128)(2,1)S(1)}, u32[]{:S(2)}, u32[]{:S(2)}) %all-to-all-start) | async-done | bytes 327712 | tf_op jit(solution)/shard_map/all_to_all | solution.py:327
  37.6 0.1 copy.11
  37.7 0.1 copy.12
  37.8 0.0 copy-start.3
  37.8 0.1 copy.19
  37.9 0.3 copy.13
  38.2 0.5 maximum_maximum_fusion.own
  38.7 1.9 %collective-permute-start.1 = (bf16[2048,128]{1,0:T(8,128)(2,1)S(1)}, bf16[2048,128]{1,0:T(8,128)(2,1)S(1)}, u32[]{:S(2)}, u32[]{:S(2)}) collective-permute-start(bf16[2048,128]{1,0:T(8,128)(2,1)S(1)} %maximum_maximum_fusion.own), channel_id=1, source_target_pairs={{16,0},{32,16},{48,32},{64,48},{80,64},{96,80},{112,96},{128,112},... | collective-permute-start | bytes 1572872 | tf_op jit(solution)/shard_map/ppermute | solution.py:343
  40.6 2.4 %collective-permute-start = (bf16[2048,128]{1,0:T(8,128)(2,1)S(1)}, bf16[2048,128]{1,0:T(8,128)(2,1)}, u32[]{:S(2)}, u32[]{:S(2)}) collective-permute-start(bf16[2048,128]{1,0:T(8,128)(2,1)S(1)} %maximum_maximum_fusion.own), channel_id=1, source_target_pairs={{0,16},{16,32},{32,48},{48,64},{64,80},{80,96},{96,112},{112,128},... | collective-permute-start | bytes 1572872 | tf_op jit(solution)/shard_map/ppermute | solution.py:342
  43.1 0.1 broadcast_add_fusion
  43.1 0.1 copy.16
  43.2 0.1 reshape.53
  43.3 0.6 reshape.50.lists
  43.9 3.0 %deviations.1 = (bf16[96,80,128]{2,1,0:T(8,128)(2,1)S(1)}, f32[96,128]{1,0:T(8,128)S(1)}) custom-call(bf16[80,96,128]{2,1,0:T(8,128)(2,1)} %ens), custom_call_target="tpu_custom_call" | custom-call | tf_op jit(solution)/shard_map/deviations/pallas_call | solution.py:201
  47.0 1.3 copy-done.1
  48.2 0.7 dynamic-slice_convert_fusion.loc
  49.0 4.4 %collective-permute-done.left = bf16[2048,128]{1,0:T(8,128)(2,1)} collective-permute-done((bf16[2048,128]{1,0:T(8,128)(2,1)S(1)}, bf16[2048,128]{1,0:T(8,128)(2,1)}, u32[]{:S(2)}, u32[]{:S(2)}) %collective-permute-start) | collective-permute-done | bytes 524320 | tf_op jit(solution)/shard_map/ppermute | solution.py:342
  53.4 18.0 %transforms.1 = bf16[384,128]{1,0:T(8,128)(2,1)S(1)} custom-call(s32[3072]{0:T(1024)} %reshape.50.lists, f32[12,256]{1,0:T(8,128)S(1)} %dynamic-slice_convert_fusion.loc, bf16[2048,128]{1,0:T(8,128)(2,1)} %collective-permute-done.left, bf16[2048,128]{1,0:T(8,128)(2,1)S(1)} %maximum_maximum_fusion.own, bf16[2048,128]{1,0:T(8,128)(2,1)S(1)} %collective-permute-done.1.right), custom_call_target="tpu_custom_call" | custom-call | tf_op jit(solution)/shard_map/transforms/pallas_call | solution.py:141
  71.4 21.6 %all_to_all.15 = bf16[16,24,128]{2,1,0:T(8,128)(2,1)S(1)} all-to-all(bf16[16,24,128]{2,1,0:T(8,128)(2,1)S(1)} %bitcast.28), channel_id=1, replica_groups=mesh['space'=32,'member'=16] {'member'}, dimensions={0} | all-to-all | bytes 196608 | tf_op jit(solution)/shard_map/all_to_all | solution.py:359
  93.0 1.1 fusion.1
  94.1 7.3 %all-to-all-start.2 = ((bf16[32,32,128]{2,1,0:T(8,128)(2,1)}), bf16[32,32,128]{2,1,0:T(8,128)(2,1)S(1)}, u32[]{:S(2)}, u32[]{:S(2)}) async-start(bf16[32,32,128]{2,1,0:T(8,128)(2,1)} %bitcast.8), calls=%async_computation.2 | async-start | bytes 524288 | tf_op jit(solution)/shard_map/all_to_all | solution.py:368
  101.5 0.1 broadcast_subtract_fusion
  101.5 0.1 fusion.14
  101.6 6.7 %all-to-all-done.2 = bf16[32,32,128]{2,1,0:T(8,128)(2,1)S(1)} async-done(((bf16[32,32,128]{2,1,0:T(8,128)(2,1)}), bf16[32,32,128]{2,1,0:T(8,128)(2,1)S(1)}, u32[]{:S(2)}, u32[]{:S(2)}) %all-to-all-start.2) | async-done | bytes 262176 | tf_op jit(solution)/shard_map/all_to_all | solution.py:368
  108.4 0.7 convolution_convert_fusion
  109.1 32.4 %all_gather.3 = bf16[3072,128]{1,0:T(8,128)(2,1)S(1)} all-gather(bf16[192,128]{1,0:T(8,128)(2,1)S(1)} %convolution_convert_fusion), channel_id=1, replica_groups=mesh['space'=32,'member'=16] {'member'}, dimensions={0}, use_global_device_ids=true | all-gather | bytes 835584 | tf_op jit(solution)/shard_map/all_gather | solution.py:381
  141.5 6.2 %apply.1 = bf16[80,96,128]{2,1,0:T(8,128)(2,1)} custom-call(bf16[16,192,128]{2,1,0:T(8,128)(2,1)S(1)} %bitcast.27, bf16[96,80,128]{2,1,0:T(8,128)(2,1)S(1)} %copy-done.2, f32[96,128]{1,0:T(8,128)S(1)} %get-tuple-element.40.mean), custom_call_target="tpu_custom_call" | custom-call | tf_op jit(solution)/shard_map/apply/pallas_call | solution.py:293
  (16 shorter events, 0.1 us)
Async XLA Ops:
  0.0 43.3 %copy-start = (s32[192,256]{1,0:T(8,128)S(1)}, s32[192,256]{1,0:T(8,128)}, u32[]{:S(2)}) copy-start(s32[192,256]{1,0:T(8,128)} %param.12) | copy-start | bytes 589828
  1.6 36.1 %all-to-all-start = ((bf16[16,80,128]{2,1,0:T(8,128)(2,1)}), bf16[16,80,128]{2,1,0:T(8,128)(2,1)S(1)}, u32[]{:S(2)}, u32[]{:S(2)}) async-start(bf16[16,80,128]{2,1,0:T(8,128)(2,1)} %copies.1), calls=%async_computation | async-start | bytes 655360 | tf_op jit(solution)/shard_map/all_to_all | solution.py:327
  37.8 5.3 %copy-start.3 = (s32[1,16,32]{2,1,0:T(8,128)S(1)}, s32[1,16,32]{2,1,0:T(8,128)}, u32[]{:S(2)}) copy-start(s32[1,16,32]{2,1,0:T(8,128)} %param.14) | copy-start | bytes 6148
  38.7 10.3 %collective-permute-start.1 = (bf16[2048,128]{1,0:T(8,128)(2,1)S(1)}, bf16[2048,128]{1,0:T(8,128)(2,1)S(1)}, u32[]{:S(2)}, u32[]{:S(2)}) collective-permute-start(bf16[2048,128]{1,0:T(8,128)(2,1)S(1)} %maximum_maximum_fusion.own), channel_id=1, source_target_pairs={{16,0},{32,16},{48,32},{64,48},{80,64},{96,80},{112,96},{128,112},... | collective-permute-start | bytes 1572872 | tf_op jit(solution)/shard_map/ppermute | solution.py:343
  40.6 12.7 %collective-permute-start = (bf16[2048,128]{1,0:T(8,128)(2,1)S(1)}, bf16[2048,128]{1,0:T(8,128)(2,1)}, u32[]{:S(2)}, u32[]{:S(2)}) collective-permute-start(bf16[2048,128]{1,0:T(8,128)(2,1)S(1)} %maximum_maximum_fusion.own), channel_id=1, source_target_pairs={{0,16},{16,32},{32,48},{48,64},{64,80},{80,96},{96,112},{112,128},... | collective-permute-start | bytes 1572872 | tf_op jit(solution)/shard_map/ppermute | solution.py:342
  46.9 1.3 copy-start.1
  48.2 53.2 %copy-start.4 = (s32[96,2]{0,1:T(2,128)S(1)}, s32[96,2]{0,1:T(2,128)}, u32[]{:S(2)}) copy-start(s32[96,2]{0,1:T(2,128)} %param.15) | copy-start | bytes 2308
  48.2 53.2 %copy-start.5 = (f32[96]{0:T(128)S(1)}, f32[96]{0:T(128)}, u32[]{:S(2)}) copy-start(f32[96]{0:T(128)} %param.16) | copy-start | bytes 1156
  71.4 70.1 %copy-start.2 = (bf16[96,80,128]{2,1,0:T(8,128)(2,1)S(1)}, bf16[96,80,128]{2,1,0:T(8,128)(2,1)}, u32[]{:S(2)}) copy-start(bf16[96,80,128]{2,1,0:T(8,128)(2,1)} %copy-done.1) | copy-start | bytes 5898244
  94.1 14.2 %all-to-all-start.2 = ((bf16[32,32,128]{2,1,0:T(8,128)(2,1)}), bf16[32,32,128]{2,1,0:T(8,128)(2,1)S(1)}, u32[]{:S(2)}, u32[]{:S(2)}) async-start(bf16[32,32,128]{2,1,0:T(8,128)(2,1)} %bitcast.8), calls=%async_computation.2 | async-start | bytes 524288 | tf_op jit(solution)/shard_map/all_to_all | solution.py:368
